TPU v7x, 16 devices: a whole 2x2x2 slice. The times are simulated.
16 devices in a mesh: dp: 4 (over z, y), tp: 4 (over x, core).
Axes of the slice: x: 2, y: 2, z: 2, core: 2. Of those that a mesh axis runs over, the one named last changes fastest.
Arguments:
- x_chunk: bfloat16 [16, 1024, 2048], P('dp', 'tp'), parts along dimension 0
- prefix_len: int32 [16], P('dp'), parts along dimension 0
- k_cache: bfloat16 [16, 4096, 16, 128], P('dp', None, 'tp'), parts along dimension 0
- v_cache: bfloat16 [16, 4096, 16, 128], P('dp', None, 'tp'), parts along dimension 0
- ln1_gain: bfloat16 [2048], replicated
- ln1_bias: bfloat16 [2048], replicated
- w_qkv: bfloat16 [2048, 6144], P(None, 'tp')
- b_qkv: bfloat16 [6144], P('tp')
- w_out: bfloat16 [2048, 2048], P('tp')
- b_out: bfloat16 [2048], replicated
- ln2_gain: bfloat16 [2048], replicated
- ln2_bias: bfloat16 [2048], replicated
- w_up: bfloat16 [2048, 8192], P(None, 'tp')
- b_up: bfloat16 [8192], P('tp')
- w_down: bfloat16 [8192, 2048], P('tp')
- b_down: bfloat16 [2048], replicated
Outputs:
- output 1: bfloat16 [16, 1024, 2048], P('dp', 'tp'), parts along dimension 0
- output 2: bfloat16 [16, 4096, 16, 128], P('dp', None, 'tp'), parts along dimension 0
- output 3: bfloat16 [16, 4096, 16, 128], P('dp', None, 'tp'), parts along dimension 0
There are 4 independent parts. A program takes and returns all parts, laid end to end along the dimension named above; an argument that names none is the same for every part.
All inputs are finite; a program needn't handle non-finite values.
Results may differ from a plain program's by a relative error of at most 0.0119016.
Values are sent between devices in bfloat16 or wider.
A program may use at most 1 GiB of HBM per device.

v0:
```python
import jax
import jax.numpy as jnp
from jax import lax
from jax.sharding import PartitionSpec as P

LN_EPS = 1e-5


def layer_norm(tok_rows, ln_gain, ln_bias):
    rows_f32 = tok_rows.astype(jnp.float32)
    row_mean = jnp.mean(rows_f32, axis=-1, keepdims=True)
    centered = rows_f32 - row_mean
    row_var = jnp.mean(centered * centered, axis=-1, keepdims=True)
    normed = centered * lax.rsqrt(row_var + LN_EPS)
    return (normed * ln_gain.astype(jnp.float32) + ln_bias.astype(jnp.float32)).astype(jnp.bfloat16)


def write_rows(cache_seq, new_rows, start_pos):
    zero_idx = jnp.zeros_like(start_pos)
    return lax.dynamic_update_slice(cache_seq, new_rows, (start_pos, zero_idx, zero_idx))


def attend(queries, k_upd, v_upd, prefix_len, head_offset, heads_all):
    batch_n, chunk_len, heads_loc, head_dim = queries.shape
    cache_len = k_upd.shape[1]
    scores = jnp.einsum('bchd,bthd->bhct', queries, k_upd, preferred_element_type=jnp.float32) * (head_dim ** -0.5)
    head_ids = head_offset + jnp.arange(heads_loc)
    slopes = jnp.exp2(-8.0 * (head_ids + 1).astype(jnp.float32) / heads_all)
    query_pos = prefix_len[:, None] + jnp.arange(chunk_len)[None, :]
    rel_pos = (jnp.arange(cache_len)[None, None, :] - query_pos[:, :, None]).astype(jnp.float32)
    scores = scores + slopes[None, :, None, None] * rel_pos[:, None]
    scores = jnp.where((rel_pos <= 0.0)[:, None], scores, -1e30)
    attn_probs = jax.nn.softmax(scores, axis=-1).astype(jnp.bfloat16)
    context = jnp.einsum('bhct,bthd->bchd', attn_probs, v_upd, preferred_element_type=jnp.float32)
    return context.astype(jnp.bfloat16).reshape(batch_n, chunk_len, heads_loc * head_dim)


def solution(mesh):
    tp_size = mesh.shape['tp']

    def local_layer(x_local, prefix_len, k_cache, v_cache, ln1_gain, ln1_bias, w_qkv, b_qkv, w_out, b_out, ln2_gain, ln2_bias, w_up, b_up, w_down, b_down):
        batch_n, tok_loc = x_local.shape[0], x_local.shape[1]
        heads_loc, head_dim = k_cache.shape[2], k_cache.shape[3]
        chunk_len = tok_loc * tp_size
        normed = layer_norm(x_local, ln1_gain, ln1_bias)
        gathered = lax.all_gather(normed, 'tp', axis=1, tiled=True)
        qkv_proj = jnp.einsum('bcd,de->bce', gathered, w_qkv, preferred_element_type=jnp.float32) + b_qkv.astype(jnp.float32)
        qkv_heads = qkv_proj.astype(jnp.bfloat16).reshape(batch_n, chunk_len, heads_loc, 3, head_dim)
        k_upd = jax.vmap(write_rows)(k_cache, qkv_heads[:, :, :, 1], prefix_len)
        v_upd = jax.vmap(write_rows)(v_cache, qkv_heads[:, :, :, 2], prefix_len)
        head_offset = lax.axis_index('tp') * heads_loc
        context = attend(qkv_heads[:, :, :, 0], k_upd, v_upd, prefix_len, head_offset, heads_loc * tp_size)
        attn_part = jnp.einsum('bce,ed->bcd', context, w_out, preferred_element_type=jnp.float32).astype(jnp.bfloat16)
        attn_sum = lax.psum_scatter(attn_part, 'tp', scatter_dimension=1, tiled=True)
        residual = (x_local.astype(jnp.float32) + attn_sum.astype(jnp.float32) + b_out.astype(jnp.float32)).astype(jnp.bfloat16)
        normed2 = layer_norm(residual, ln2_gain, ln2_bias)
        gathered2 = lax.all_gather(normed2, 'tp', axis=1, tiled=True)
        up_pre = jnp.einsum('bcd,df->bcf', gathered2, w_up, preferred_element_type=jnp.float32) + b_up.astype(jnp.float32)
        up_act = jax.nn.gelu(up_pre, approximate=True).astype(jnp.bfloat16)
        down_part = jnp.einsum('bcf,fd->bcd', up_act, w_down, preferred_element_type=jnp.float32).astype(jnp.bfloat16)
        down_sum = lax.psum_scatter(down_part, 'tp', scatter_dimension=1, tiled=True)
        x_out = (residual.astype(jnp.float32) + down_sum.astype(jnp.float32) + b_down.astype(jnp.float32)).astype(jnp.bfloat16)
        return x_out, k_upd, v_upd

    tok_spec = P('dp', 'tp', None)
    cache_spec = P('dp', None, 'tp', None)
    replicated = P()
    in_specs = (tok_spec, P('dp'), cache_spec, cache_spec, replicated, replicated, P(None, 'tp'), P('tp'), P('tp', None), replicated, replicated, replicated, P(None, 'tp'), P('tp'), P('tp', None), replicated)
    return jax.shard_map(local_layer, mesh=mesh, in_specs=in_specs, out_specs=(tok_spec, cache_spec, cache_spec), check_vma=False)
```

profile of v0, /device:TPU:0, one launch (start us, length us, event | category | flops | bytes accessed | tf_op | source)
XLA Modules:
  0.0 1080.4 jit_solution(2912487902767965692)
XLA Ops:
  7.2 12.1 %copy.82 = bf16[4,4096,4,128]{3,2,1,0:T(4,128)(2,1)} copy(bf16[4,4096,4,128]{3,2,1,0:T(4,128)(2,1)} %param.18) | data formatting | bytes 33554432
  19.3 13.4 %copy.83 = bf16[4,4096,4,128]{3,2,1,0:T(4,128)(2,1)} copy(bf16[4,4096,4,128]{3,2,1,0:T(4,128)(2,1)} %param.19) | data formatting | bytes 33554432
  33.4 1.2 fusion.45
  34.7 3.1 fusion.48
  38.6 21.3 %subtract_convert_fusion = f32[4,1024,4096]{2,1,0:T(8,128)} fusion(s32[4,1024]{1,0:T(4,128)S(1)} %iota_add_fusion), kind=kLoop, calls=%fused_computation.21 | loop fusion | flops 33554432 | bytes 67125248 | tf_op jit(solution)/shard_map/convert_element_type | solution.py:30
  59.9 15.4 %broadcast_compare_fusion = pred[4,1024,4096]{2,1,0:T(8,128)(4,1)} fusion(s32[4,1024]{1,0:T(4,128)S(1)} %iota_add_fusion), kind=kLoop, calls=%fused_computation.31 | loop fusion | flops 50331648 | bytes 16793600 | tf_op jit(solution)/shard_map/le | solution.py:32
  75.4 70.5 %all-gather.3.cloned.1.call-done = bf16[4,1024,2048]{2,1,0:T(8,128)(2,1)} async-done(((bf16[4,256,2048]{2,1,0:T(8,128)(2,1)}), bf16[4,1024,2048]{2,1,0:T(8,128)(2,1)}) %all-gather.3.cloned.1.call-update) | async-done | bytes 16777232 | tf_op jit(solution)/shard_map/all_gather | solution.py:46
  145.8 32.4 %add_convert_fusion = bf16[4,1024,1536]{2,1,0:T(8,128)(2,1)} fusion(bf16[4,1024,2048]{2,1,0:T(8,128)(2,1)} %all-gather.3.cloned.1.call-done, f32[1536]{0:T(1024)S(1)} %convert_element_type.92, bf16[2048,1536]{1,0:T(8,128)(2,1)} %param.22), kind=kOutput, calls=%fused_computation.33 | convolution fusion | flops 25782386688 | bytes 35657728 | tf_op jit(solution)/shard_map/bcd,de->bce/dot_general | solution.py:47
  178.2 16.7 %copy.27 = bf16[4,1024,1536]{1,2,0:T(8,128)(2,1)} copy(bf16[4,1024,1536]{2,1,0:T(8,128)(2,1)} %add_convert_fusion) | data formatting | bytes 25165824 | tf_op jit(solution)/shard_map/convert_element_type | solution.py:48
  194.9 6.1 slice_bitcast_fusion.2
  201.0 49.1 %while.3 = (s32[]{:T(128)}, bf16[4,4096,4,128]{3,2,1,0:T(4,128)(2,1)}, s32[4,4]{1,0:T(4,128)S(1)}, bf16[4,1024,4,128]{1,3,2,0:T(8,128)(2,1)}, s32[]{:T(128)}, /*index=5*/s32[4]{0:T(128)S(1)}) while((s32[]{:T(128)}, bf16[4,4096,4,128]{3,2,1,0:T(4,128)(2,1)}, s32[4,4]{1,0:T(4,128)S(1)}, bf16[4,1024,4,128]{1,3,2,0:T(8,128)(2,1)}, s32[]{:T(128)}, ...), condition=%wide.while_cond.1, body=%wide.while_body.1.sunk | while | flops 524317 | bytes 7341750 | solution.py:20
  201.7 3.2 and_reduce_fusion.5
  204.9 2.3 constant_dynamic-slice_fusion.11
  207.1 1.7 copy.65
  208.8 4.5 fusion.102
  213.3 0.7 fusion.101
  214.0 3.2 and_reduce_fusion.5
  217.1 2.3 constant_dynamic-slice_fusion.11
  219.4 1.7 copy.65
  221.1 4.5 fusion.102
  225.6 0.7 fusion.101
  226.3 3.2 and_reduce_fusion.5
  229.4 2.3 constant_dynamic-slice_fusion.11
  231.7 1.7 copy.65
  233.4 4.5 fusion.102
  237.9 0.7 fusion.101
  238.5 3.2 and_reduce_fusion.5
  241.7 2.3 constant_dynamic-slice_fusion.11
  244.0 1.7 copy.65
  245.7 4.5 fusion.102
  250.1 50.2 %while.2 = (s32[]{:T(128)}, bf16[4,4096,4,128]{3,2,1,0:T(4,128)(2,1)}, s32[4,4]{1,0:T(4,128)S(1)}, bf16[4,1024,4,128]{1,3,2,0:T(8,128)(2,1)}, s32[]{:T(128)}, /*index=5*/s32[4]{0:T(128)S(1)}) while((s32[]{:T(128)}, bf16[4,4096,4,128]{3,2,1,0:T(4,128)(2,1)}, s32[4,4]{1,0:T(4,128)S(1)}, bf16[4,1024,4,128]{1,3,2,0:T(8,128)(2,1)}, s32[]{:T(128)}, ...), condition=%wide.while_cond, body=%wide.while_body.sunk | while | flops 524317 | bytes 7341750 | solution.py:20
  250.1 0.7 fusion.99
  250.8 3.2 and_reduce_fusion.4
  254.0 2.4 constant_dynamic-slice_fusion.9
  256.4 1.7 copy.64
  258.1 4.6 fusion.100
  262.7 0.7 fusion.99
  263.4 3.2 and_reduce_fusion.4
  266.6 2.4 constant_dynamic-slice_fusion.9
  268.9 1.7 copy.64
  270.7 4.6 fusion.100
  275.2 0.7 fusion.99
  275.9 3.2 and_reduce_fusion.4
  279.1 2.4 constant_dynamic-slice_fusion.9
  281.5 1.7 copy.64
  283.2 4.6 fusion.100
  287.8 0.7 fusion.99
  288.5 3.2 and_reduce_fusion.4
  291.7 2.4 constant_dynamic-slice_fusion.9
  294.1 1.7 copy.64
  295.8 4.6 fusion.100
  300.3 137.9 %fusion.78 = f32[4,4,1024]{2,1,0:T(4,128)S(1)} fusion(f32[4,1024,4096]{2,1,0:T(8,128)} %subtract_convert_fusion, f32[4]{0:T(128)S(1)} %multiply_exponential_fusion, pred[4,1024,4096]{2,1,0:T(8,128)(4,1)} %broadcast_compare_fusion, bf16[4,4096,4,128]{3,2,1,0:T(4,128)(2,1)} %get-tuple-element.16, bf16[4,1024,4,3,128]{1,4,3,2,0:T(8,128)(2,1)} %bitcast.86), kind=kOutput, calls=%fused_computation.98 | convolution fusion | flops 17582526464 | bytes 104923152 | tf_op jit(solution)/shard_map/sub | solution.py:33
  438.3 166.7 %fusion.57 = bf16[4,4,128,1024]{3,2,1,0:T(8,128)(2,1)} fusion(f32[4,4,1024]{2,1,0:T(4,128)S(1)} %fusion.78, f32[4,1024,4096]{2,1,0:T(8,128)} %subtract_convert_fusion, f32[4]{0:T(128)S(1)} %multiply_exponential_fusion, pred[4,1024,4096]{2,1,0:T(8,128)(4,1)} %broadcast_compare_fusion, bf16[4,4096,4,128]{3,2,1,0:T(4,128)(2,1)} %get-tuple-element.16, ...), kind=kOutput, calls=%fused_computation.75 | convolution fusion | flops 34831618048 | bytes 125894672 | tf_op jit(solution)/shard_map/bhct,bthd->bchd/dot_general | solution.py:34
  605.0 14.9 %convolution_convert_fusion = bf16[4,1024,2048]{2,1,0:T(8,128)(2,1)} fusion(bf16[4,1024,512]{1,2,0:T(8,128)(2,1)} %bitcast.88, bf16[512,2048]{1,0:T(8,128)(2,1)S(1)} %copy-done), kind=kOutput, calls=%fused_computation.42 | convolution fusion | flops 8598323200 | bytes 23068672 | tf_op jit(solution)/shard_map/bce,ed->bcd/dot_general | solution.py:53
  620.6 120.0 %reduce-scatter.3.cloned.1.call-done = bf16[4,256,2048]{2,1,0:T(8,128)(2,1)} async-done(((bf16[4,1024,2048]{2,1,0:T(8,128)(2,1)}), bf16[4,256,2048]{2,1,0:T(8,128)(2,1)}) %reduce-scatter.3.cloned.1.call-update) | async-done | bytes 4194320 | tf_op jit(solution)/shard_map/reduce_scatter | solution.py:54
  740.6 5.5 convert_reduce_fusion
  746.1 1.2 fusion.41
  747.4 0.7 copy-done.2
  748.1 3.0 fusion.44
  751.3 105.2 %all-gather.5.cloned.1.call-done = bf16[4,1024,2048]{2,1,0:T(8,128)(2,1)} async-done(((bf16[4,256,2048]{2,1,0:T(8,128)(2,1)}), bf16[4,1024,2048]{2,1,0:T(8,128)(2,1)}) %all-gather.5.cloned.1.call-update) | async-done | bytes 16777232 | tf_op jit(solution)/shard_map/all_gather | solution.py:57
  856.5 46.3 %fusion.17.clone.6 = bf16[4,1024,2048]{2,1,0:T(8,128)(2,1)S(1)} fusion(bf16[4,1024,2048]{2,1,0:T(8,128)(2,1)} %all-gather.5.cloned.1.call-done, f32[2048]{0:T(1024)S(1)} %convert_element_type.107, bf16[2048,2048]{1,0:T(8,128)(2,1)} %param.28), kind=kOutput, calls=%fused_computation.30.clone.clone.clone.clone.clone.1 | convolution fusion | flops 34443624448 | bytes 41951232 | tf_op jit(solution)/shard_map/bcd,df->bcf/dot_general | solution.py:58
  902.8 42.1 %fusion.27 = bf16[4,1024,2048]{2,1,0:T(8,128)(2,1)} fusion(bf16[2048,2048]{1,0:T(8,128)(2,1)} %param.30, bf16[4,1024,2048]{2,1,0:T(8,128)(2,1)S(1)} %fusion.17.clone.6), kind=kOutput, calls=%fused_computation.41 | convolution fusion | flops 34368126976 | bytes 41943040 | tf_op jit(solution)/shard_map/bcf,fd->bcd/dot_general | solution.py:60
  945.5 120.0 %reduce-scatter.5.cloned.1.call-done = bf16[4,256,2048]{2,1,0:T(8,128)(2,1)} async-done(((bf16[4,1024,2048]{2,1,0:T(8,128)(2,1)}), bf16[4,256,2048]{2,1,0:T(8,128)(2,1)}) %reduce-scatter.5.cloned.1.call-update) | async-done | bytes 4194320 | tf_op jit(solution)/shard_map/reduce_scatter | solution.py:61
  1065.6 7.9 fusion.52
  (64 shorter events, 3.8 us)
Async XLA Ops:
  7.2 597.9 %copy-start = (bf16[512,2048]{1,0:T(8,128)(2,1)S(1)}, bf16[512,2048]{1,0:T(8,128)(2,1)}, u32[]{:S(2)}) copy-start(bf16[512,2048]{1,0:T(8,128)(2,1)} %param.24) | copy-start | bytes 6291460
  7.2 138.7 %all-gather.3.cloned.1.call-start = ((), (), s32[]{:S(2)}) async-start(), calls=%async_computation.2 | async-start | bytes 20971520 | tf_op jit(solution)/shard_map/all_gather | solution.py:46
  19.3 13.4 %copy-start.1 = (bf16[4,256,2048]{2,1,0:T(8,128)(2,1)S(1)}, bf16[4,256,2048]{2,1,0:T(8,128)(2,1)}, u32[]{:S(2)}) copy-start(bf16[4,256,2048]{2,1,0:T(8,128)(2,1)} %param.16) | copy-start | bytes 12582916
  19.3 15.3 %copy-start.4 = (bf16[2048]{0:T(1024)(128)(2,1)S(1)}, bf16[2048]{0:T(1024)(128)(2,1)}, u32[]{:S(2)}) copy-start(bf16[2048]{0:T(1024)(128)(2,1)} %param.20) | copy-start | bytes 12292
  19.3 15.3 %copy-start.5 = (bf16[2048]{0:T(1024)(128)(2,1)S(1)}, bf16[2048]{0:T(1024)(128)(2,1)}, u32[]{:S(2)}) copy-start(bf16[2048]{0:T(1024)(128)(2,1)} %param.21) | copy-start | bytes 12292
  32.7 5.6 copy-start.12
  32.7 5.6 copy-start.13
  32.7 5.8 copy-start.6
  37.7 702.9 %reduce-scatter.3.cloned.1.call-start = ((), (), s32[]{:S(2)}) async-start(), calls=%async_computation.3 | async-start | bytes 20971520 | tf_op jit(solution)/shard_map/reduce_scatter | solution.py:54
  178.2 22.8 %copy-start.3 = (s32[4]{0:T(128)S(1)}, s32[4]{0:T(128)}, u32[]{:S(2)}) copy-start(s32[4]{0:T(128)} %constant.155) | copy-start | bytes 52
  619.9 0.7 copy-start.7
  619.9 0.7 copy-start.8
  619.9 0.7 copy-start.9
  619.9 131.4 %copy-start.10 = (bf16[2048]{0:T(1024)(128)(2,1)S(1)}, bf16[2048]{0:T(1024)(128)(2,1)}, u32[]{:S(2)}) copy-start(bf16[2048]{0:T(1024)(128)(2,1)} %param.29) | copy-start | bytes 12292
  619.9 236.5 %all-gather.5.cloned.1.call-start = ((), (), s32[]{:S(2)}) async-start(), calls=%async_computation.4 | async-start | bytes 20971520 | tf_op jit(solution)/shard_map/all_gather | solution.py:57
  746.1 2.0 copy-start.2
  751.2 314.4 %reduce-scatter.5.cloned.1.call-start = ((), (), s32[]{:S(2)}) async-start(), calls=%async_computation.5 | async-start | bytes 20971520 | tf_op jit(solution)/shard_map/reduce_scatter | solution.py:61
  944.8 0.7 copy-start.11
Sparse Core Ops, SparseCore 0:
  37.9 107.9 all-gather.2
  620.0 120.5 reduce-scatter.2
  751.3 105.0 all-gather.4
  945.0 120.5 reduce-scatter.4
where the time goes:
time: 1090 us; the launch traced here: 1080 us
  matrix products  440 us (40%)
  waiting for transfers between devices  416 us (38%)
  other arithmetic  121 us (11%)
  local copies, waits for them, and re-layouts  87.9 us (8%)
  between operations  14.5 us (1%)
    dot_general x1, matrix products, attend(): jnp.einsum('bhct,bthd->bchd', attn_probs, v_upd, preferred_element_type=j...  167 us
    sub x1, matrix products, attend(): attn_probs = jax.nn.softmax(scores, axis=-1).astype(jnp.bfloat16)  138 us
    reduce_scatter x1, waiting for transfers between devices, local_layer(): lax.psum_scatter(attn_part, 'tp', scatter_dimension=1, tiled=True)  120 us
    reduce_scatter x1, waiting for transfers between devices, local_layer(): lax.psum_scatter(down_part, 'tp', scatter_dimension=1, tiled=True)  120 us
    all_gather x1, waiting for transfers between devices, local_layer(): gathered2 = lax.all_gather(normed2, 'tp', axis=1, tiled=True)  105 us
    all_gather x1, waiting for transfers between devices, local_layer(): gathered = lax.all_gather(normed, 'tp', axis=1, tiled=True)  70.5 us
    scatter x16, other arithmetic  61.7 us
    dot_general x1, matrix products, local_layer(): jnp.einsum('bcd,df->bcf', gathered2, w_up, preferred_element_type=jnp.flo...  46.3 us
  transfers between devices with their start and end apart: 4, of which 4 were waited for; matrix products, arithmetic and copies ran while one was open for 3% of the time, Pallas kernels for 0%

commit v1 on v0

v1 whole, which is shorter than its diff:
```python
import functools

import jax
import jax.numpy as jnp
from jax import lax
from jax.experimental import pallas as pl
from jax.experimental.pallas import tpu as pltpu
from jax.sharding import PartitionSpec as P


LN_EPS = 1e-5
LOG2E = 1.4426950408889634
MASKED = -1e30 * LOG2E
F32 = jnp.float32
BF16 = jnp.bfloat16
QB = 512
KB = 512
PREP_TOK = 1024
MLP_ROWS = 512
QKV_GROUP = 2
VMEM_BIG = 60 * 1024 * 1024


def ln_rows(rows, gain, bias):
    rows = rows.astype(F32)
    mean = jnp.mean(rows, axis=-1, keepdims=True)
    centered = rows - mean
    var = jnp.mean(centered * centered, axis=-1, keepdims=True)
    return (centered * lax.rsqrt(var + LN_EPS) * gain + bias).astype(BF16)


def prep_kernel(heads, len_ref, k_ref, v_ref, ko_ref, vo_ref, kt_ref, vt_ref, ks, vs):
    toks = kt_ref.shape[2]
    ko_ref[...] = k_ref[...]
    vo_ref[...] = v_ref[...]

    @pl.when(pl.program_id(1) * toks < len_ref[pl.program_id(0)])
    def _():
        for src, tr, tmp in ((k_ref, kt_ref, ks), (v_ref, vt_ref, vs)):
            tmp[...] = src[0].astype(F32)
            for h in range(heads):
                tr[0, h] = tmp[pl.ds(h, toks, stride=heads), :].astype(BF16)


def prep(lens, kc, vc, heads):
    seqs, rows, hd = kc.shape
    toks = rows // heads
    flat = pl.BlockSpec((1, PREP_TOK * heads, hd), lambda b, j, s: (b, j, 0))
    last = lambda b, s: jnp.maximum((s[b] + PREP_TOK - 1) // PREP_TOK, 1) - 1
    tr = pl.BlockSpec((1, heads, PREP_TOK, hd), lambda b, j, s: (b, 0, jnp.minimum(j, last(b, s)), 0))
    flat_t = jax.ShapeDtypeStruct(kc.shape, BF16)
    tr_t = jax.ShapeDtypeStruct((seqs, heads, toks, hd), BF16)
    return pl.pallas_call(
        functools.partial(prep_kernel, heads),
        grid_spec=pltpu.PrefetchScalarGridSpec(
            num_scalar_prefetch=1,
            grid=(seqs, toks // PREP_TOK),
            in_specs=[flat, flat],
            out_specs=[flat, flat, tr, tr],
            scratch_shapes=[pltpu.VMEM((PREP_TOK * heads, hd), F32)] * 2,
        ),
        out_shape=[flat_t, flat_t, tr_t, tr_t],
        compiler_params=pltpu.CompilerParams(vmem_limit_bytes=VMEM_BIG),
        cost_estimate=pl.CostEstimate(flops=int(2e10), bytes_accessed=kc.size * 12, transcendentals=0),
        name="prep",
    )(lens, kc, vc)


def row_of(ref, n=None):
    vec = ref[...] if n is None else ref[n]
    return vec.astype(F32).reshape(1, -1)


def ln1_kernel(seqs, x_ref, g_ref, lb_ref, bu_ref, up_ref, down_ref, wo_ref, *refs):
    outs, (upq, downq, buf, ub, db, sems, isems, osems) = refs[:seqs], refs[seqs:]
    seq = pl.program_id(0)
    dp = lax.axis_index("dp")
    feats, width = up_ref.shape[0], ub.shape[1]
    few = db.shape[0] - width
    cols = lambda n: pl.ds(pl.multiple_of(dp * n, n), n)
    ins = [pltpu.make_async_copy(up_ref.at[:, cols(width)], ub.at[:feats], isems.at[0]),
           pltpu.make_async_copy(down_ref.at[cols(width)], db.at[:width], isems.at[1]),
           pltpu.make_async_copy(wo_ref.at[cols(few)], db.at[width:], isems.at[2])]
    packs = [pltpu.make_async_copy(ub, upq, osems.at[0]), pltpu.make_async_copy(db, downq, osems.at[1])]

    @pl.when(seq == 0)
    def _():
        for copy in ins:
            copy.start()
        ub[feats:, :] = jnp.broadcast_to(row_of(bu_ref, cols(width)), (ub.shape[0] - feats, width)).astype(BF16)

    normed = ln_rows(x_ref[0], row_of(g_ref), row_of(lb_ref))
    for n in range(seqs):
        @pl.when(seq == n)
        def _(n=n):
            buf[n] = normed
            pltpu.make_async_copy(buf.at[n], outs[n], sems.at[n]).start()

    @pl.when(seq == seqs - 1)
    def _():
        for copy in ins:
            copy.wait()
        for copy in packs:
            copy.start()
        for n in range(seqs):
            pltpu.make_async_copy(buf.at[n], outs[n], sems.at[n]).wait()
        for copy in packs:
            copy.wait()


def ln1(x, g, b, bu, w_up, w_down, w_out, parts):
    seqs, tok, feats = x.shape
    up_t = jax.ShapeDtypeStruct((feats + 16, w_up.shape[1] // parts), BF16)
    down_t = jax.ShapeDtypeStruct(((w_down.shape[0] + w_out.shape[0]) // parts, feats), BF16)
    hbm = pl.BlockSpec(memory_space=pl.ANY)
    return pl.pallas_call(
        functools.partial(ln1_kernel, seqs),
        grid=(seqs,),
        in_specs=[pl.BlockSpec((1, tok, feats), lambda n: (n, 0, 0)), *[pl.BlockSpec(v.shape, lambda n: (0,)) for v in (g, b, bu)], hbm, hbm, hbm],
        out_specs=[hbm] * (seqs + 2),
        out_shape=[jax.ShapeDtypeStruct((tok, feats), BF16)] * seqs + [up_t, down_t],
        scratch_shapes=[pltpu.VMEM((seqs, tok, feats), BF16), pltpu.VMEM(up_t.shape, BF16), pltpu.VMEM(down_t.shape, BF16),
                        pltpu.SemaphoreType.DMA((seqs,)), pltpu.SemaphoreType.DMA((3,)), pltpu.SemaphoreType.DMA((2,))],
        compiler_params=pltpu.CompilerParams(vmem_limit_bytes=VMEM_BIG),
        cost_estimate=pl.CostEstimate(flops=int(2e9), bytes_accessed=x.size * 8, transcendentals=0),
        name="ln1",
    )(x, g, b, bu, w_up, w_down, w_out)


def qkv_kernel(heads, hd, group, idx_ref, p0, p1, p2, p3, w_ref, b_ref,
               q_ref, k_ref, v_ref, ki_ref, vi_ref, norm_s, ks, vs, sems):
    step = pl.program_id(0)
    chunk = norm_s.shape[0]
    toks = chunk // 4

    @pl.when(step == 0)
    def _():
        copies = []
        for n, piece in enumerate((p0, p1, p2, p3)):
            at = pl.ds(pl.multiple_of((idx_ref[0] ^ n) * toks, toks), toks)
            copies.append(pltpu.make_async_copy(piece, norm_s.at[at], sems.at[n]))
        for copy in copies:
            copy.start()
        for copy in copies:
            copy.wait()

    bias = row_of(b_ref)
    bias = jnp.where(step == 0, bias[:, :w_ref.shape[1]], bias[:, w_ref.shape[1]:])
    out = jnp.dot(norm_s[...], w_ref[...], preferred_element_type=F32) + bias
    for n in range(group):
        c0 = n * 3 * hd
        k = out[:, c0 + hd:c0 + 2 * hd]
        v = out[:, c0 + 2 * hd:c0 + 3 * hd]
        q_ref[n] = out[:, c0:c0 + hd].astype(BF16)
        k_ref[n] = k.astype(BF16)
        v_ref[n] = v.astype(BF16)
        ks[pl.ds(step * group + n, chunk, stride=heads), :] = k
        vs[pl.ds(step * group + n, chunk, stride=heads), :] = v

    @pl.when(step == heads // group - 1)
    def _():
        ki_ref[...] = ks[...].astype(BF16)
        vi_ref[...] = vs[...].astype(BF16)


def qkv(idx, pieces, w, b, heads, hd):
    toks, feats = pieces[0].shape
    chunk = toks * len(pieces)
    group = QKV_GROUP
    wide = group * 3 * hd
    hbm = pl.BlockSpec(memory_space=pl.ANY)
    out_h = pl.BlockSpec((group, chunk, hd), lambda n, s: (n, 0, 0))
    out_i = pl.BlockSpec((chunk * heads, hd), lambda n, s: (0, 0))
    h_t = jax.ShapeDtypeStruct((heads, chunk, hd), BF16)
    i_t = jax.ShapeDtypeStruct((chunk * heads, hd), BF16)
    return pl.pallas_call(
        functools.partial(qkv_kernel, heads, hd, group),
        grid_spec=pltpu.PrefetchScalarGridSpec(
            num_scalar_prefetch=1,
            grid=(heads // group,),
            in_specs=[hbm] * 4 + [pl.BlockSpec((feats, wide), lambda n, s: (0, n)), pl.BlockSpec(b.shape, lambda n, s: (0,))],
            out_specs=[out_h, out_h, out_h, out_i, out_i],
            scratch_shapes=[pltpu.VMEM((chunk, feats), BF16)] + [pltpu.VMEM((chunk * heads, hd), F32)] * 2 + [pltpu.SemaphoreType.DMA((4,))],
        ),
        out_shape=[h_t, h_t, h_t, i_t, i_t],
        compiler_params=pltpu.CompilerParams(vmem_limit_bytes=VMEM_BIG),
        cost_estimate=pl.CostEstimate(flops=2 * chunk * feats * w.shape[1], bytes_accessed=w.size * 2 + chunk * feats * 2, transcendentals=0),
        name="qkv",
    )(idx, *pieces, w, b)


def attn_kernel(seq, heads, idx_ref, len_ref, slope_ref, q_ref, kn_ref, vn_ref, kt_ref, vt_ref, ki_ref, vi_ref,
                ko_in, vo_in, c0, c1, c2, c3, ko_ref, vo_ref, m_s, l_s, acc_s, stage, sems):
    head = pl.program_id(0)
    length = len_ref[seq]
    chunk, hd = q_ref.shape[1], q_ref.shape[2]

    def rows_in(n):
        return pltpu.make_async_copy((ki_ref, vi_ref)[n], stage.at[n], sems.at[n])

    def rows_out(n):
        return pltpu.make_async_copy(stage.at[n], (ko_ref, vo_ref)[n].at[seq, pl.ds(length, chunk)], sems.at[n])

    @pl.when(head == 0)
    def _():
        for n in range(2):
            rows_in(n).start()

    @pl.when(head == 1)
    def _():
        for n in range(2):
            rows_in(n).wait()
            rows_out(n).start()

    scale = LOG2E * hd ** -0.5
    slope = slope_ref[head] * LOG2E
    n_full = length // KB
    rest = length - n_full * KB
    tok = chunk // 4
    halves = range(chunk // QB)

    def scores(qi, k, base):
        q = q_ref[0, qi * QB:(qi + 1) * QB, :]
        s = lax.dot_general(q, k, (((1,), (1,)), ((), ())), preferred_element_type=F32) * scale
        pos = (lax.broadcasted_iota(jnp.int32, (1, KB), 1) + (base - qi * QB)).astype(F32) * slope
        return s + pos

    def lanes_sum(p):
        tot = p[:, :128]
        for n in range(1, KB // 128):
            tot = tot + p[:, n * 128:(n + 1) * 128]
        return tot

    def update(qi, s, v):
        m_prev = m_s[qi]
        m_new = jnp.maximum(m_prev, jnp.max(s, axis=1, keepdims=True))
        alpha = jnp.exp2(m_prev - m_new)
        p = jnp.exp2(s - jnp.tile(m_new, (1, KB // 128)))
        l_s[qi] = l_s[qi] * alpha + lanes_sum(p)
        acc_s[qi] = acc_s[qi] * alpha + jnp.dot(p.astype(BF16), v, preferred_element_type=F32)
        m_s[qi] = m_new

    for qi in halves:
        new = slice(qi * QB, (qi + 1) * QB)
        s = scores(qi, kn_ref[0, new, :], qi * QB)
        row = lax.broadcasted_iota(jnp.int32, (QB, KB), 0)
        col = lax.broadcasted_iota(jnp.int32, (QB, KB), 1)
        s = jnp.where(col <= row, s, MASKED)
        m_new = jnp.broadcast_to(jnp.max(s, axis=1, keepdims=True), (QB, 128))
        p = jnp.exp2(s - jnp.tile(m_new, (1, KB // 128)))
        m_s[qi] = m_new
        l_s[qi] = lanes_sum(p)
        acc_s[qi] = jnp.dot(p.astype(BF16), vn_ref[0, new, :], preferred_element_type=F32)

    for qi in halves:
        for kj in range(qi):
            blk = slice(kj * KB, (kj + 1) * KB)
            update(qi, scores(qi, kn_ref[0, blk, :], kj * KB), vn_ref[0, blk, :])

    def old_block(n, carry):
        start = pl.multiple_of(n * KB, KB)
        k, v = kt_ref[0, 0, pl.ds(start, KB), :], vt_ref[0, 0, pl.ds(start, KB), :]
        s = [scores(qi, k, start - length) for qi in halves]
        for qi in halves:
            update(qi, s[qi], v)
        return carry

    lax.fori_loop(0, n_full, old_block, 0)

    @pl.when(rest > 0)
    def _():
        start = pl.multiple_of(n_full * KB, KB)
        k, v = kt_ref[0, 0, pl.ds(start, KB), :], vt_ref[0, 0, pl.ds(start, KB), :]
        inside = lax.broadcasted_iota(jnp.int32, (QB, KB), 1) < rest
        for qi in halves:
            update(qi, jnp.where(inside, scores(qi, k, start - length), MASKED), v)

    for qi in halves:
        ctx = (acc_s[qi] / jnp.sum(l_s[qi], axis=1, keepdims=True)).astype(BF16)
        for j in range(QB // tok):
            owner = idx_ref[0] ^ (qi * (QB // tok) + j)
            for n, out in enumerate((c0, c1, c2, c3)):
                @pl.when(owner == n)
                def _(out=out, j=j, ctx=ctx):
                    out[...] = ctx[j * tok:(j + 1) * tok, :]

    @pl.when(head == heads - 1)
    def _():
        for n in range(2):
            rows_out(n).wait()


def attend(seq, idx, lens, slopes, q, kn, vn, kt, vt, ki, vi, ko, vo):
    heads, chunk, hd = q.shape
    toks = kt.shape[2]
    tok = chunk // 4
    per_head = pl.BlockSpec((1, chunk, hd), lambda h, *_: (h, 0, 0))
    old = pl.BlockSpec((1, 1, toks, hd), lambda h, *_: (seq, h, 0, 0))
    hbm = pl.BlockSpec(memory_space=pl.ANY)
    piece = pl.BlockSpec((tok, hd), lambda h, *_: (0, h))
    piece_t = jax.ShapeDtypeStruct((tok, heads * hd), BF16)
    cache_t = jax.ShapeDtypeStruct(ko.shape, BF16)
    pairs = heads * chunk * (toks // 2 + chunk // 2)
    return pl.pallas_call(
        functools.partial(attn_kernel, seq, heads),
        grid_spec=pltpu.PrefetchScalarGridSpec(
            num_scalar_prefetch=3,
            grid=(heads,),
            in_specs=[per_head] * 3 + [old, old, hbm, hbm, hbm, hbm],
            out_specs=[piece] * 4 + [hbm, hbm],
            scratch_shapes=[pltpu.VMEM((chunk // QB, QB, 128), F32), pltpu.VMEM((chunk // QB, QB, 128), F32), pltpu.VMEM((chunk // QB, QB, hd), F32), pltpu.VMEM((2, *ki.shape), BF16),
                            pltpu.SemaphoreType.DMA((2,))],
        ),
        out_shape=[piece_t] * 4 + [cache_t, cache_t],
        input_output_aliases={10: 4, 11: 5},
        compiler_params=pltpu.CompilerParams(vmem_limit_bytes=VMEM_BIG, has_side_effects=True),
        cost_estimate=pl.CostEstimate(flops=8 * pairs * hd, bytes_accessed=4 * heads * toks * hd, transcendentals=pairs),
        name="attend",
    )(idx, lens, slopes, q, kn, vn, kt, vt, ki, vi, ko, vo)


def out_kernel(seqs, far_row, *refs):
    refs = list(refs)
    take = lambda n: [refs.pop(0) for _ in range(n)]
    (idx_ref,) = take(1)
    xs, ctx = take(1)[0], [take(4) for _ in seqs]
    near, far = take(2), [take(4), take(4)]
    b_ref, g_ref, lb_ref, r_ref, n_ref, xb, cb, wb, acc, xsem, csem, wsem = refs
    tok = ctx[0][0].shape[0]
    part = near[0].shape[0]
    few = part // 4
    copies = [pltpu.make_async_copy(xs.at[pl.ds(seqs[0], len(seqs))], xb, xsem)]
    for i in range(len(seqs)):
        for k in range(4):
            copies.append(pltpu.make_async_copy(ctx[i][k], cb.at[i * tok:(i + 1) * tok, k * part:(k + 1) * part], csem.at[i, k]))
    first_w = len(copies)
    parts = [[pltpu.make_async_copy(near[a], wb.at[a * part:(a + 1) * part], wsem.at[a, 0])] for a in range(2)]
    for a in range(2):
        parts.append([])
        for n in range(4):
            at = pl.ds(pl.multiple_of((a + 2) * part + (idx_ref[1] ^ n) * few, few), few)
            parts[-1].append(pltpu.make_async_copy(far[a][n].at[far_row:far_row + few], wb.at[at], wsem.at[a + 2, n]))
    copies += [c for group in parts for c in group]
    for copy in copies:
        copy.start()
    for copy in copies[:first_w]:
        copy.wait()
    for k in range(4):
        for copy in parts[k]:
            copy.wait()
        total = jnp.dot(cb[:, k * part:(k + 1) * part], wb[k * part:(k + 1) * part, :], preferred_element_type=F32)
        acc[...] = total if k == 0 else acc[...] + total
    for i in range(len(seqs)):
        rows = slice(i * tok, (i + 1) * tok)
        res = (xb[i].astype(F32) + acc[rows, :] + row_of(b_ref)).astype(BF16)
        r_ref[rows, :] = res
        n_ref[rows, :] = ln_rows(res, row_of(g_ref), row_of(lb_ref))


def out_proj(idx, x, seqs, ctx, near, far, far_row, b, g, lb):
    tok, feats = x.shape[1:]
    rows = tok * len(seqs)
    flat = [c for got in ctx for c in got]
    vec = pl.BlockSpec(b.shape, lambda n, s: (0,))
    hbm = pl.BlockSpec(memory_space=pl.ANY)
    t = jax.ShapeDtypeStruct((rows, feats), BF16)
    out = pl.BlockSpec((rows, feats), lambda n, s: (0, 0))
    return pl.pallas_call(
        functools.partial(out_kernel, seqs, far_row),
        grid_spec=pltpu.PrefetchScalarGridSpec(
            num_scalar_prefetch=1, grid=(1,),
            in_specs=[hbm] * (1 + len(flat) + 10) + [vec] * 3, out_specs=[out, out],
            scratch_shapes=[pltpu.VMEM((len(seqs), tok, feats), BF16), pltpu.VMEM((rows, feats), BF16), pltpu.VMEM((feats, feats), BF16),
                            pltpu.VMEM((rows, feats), F32), pltpu.SemaphoreType.DMA, pltpu.SemaphoreType.DMA((len(seqs), 4)), pltpu.SemaphoreType.DMA((4, 4))],
        ),
        out_shape=[t, t],
        compiler_params=pltpu.CompilerParams(vmem_limit_bytes=VMEM_BIG),
        cost_estimate=pl.CostEstimate(flops=2 * rows * feats * feats, bytes_accessed=2 * feats * feats, transcendentals=0),
        name="outp",
    )(idx, x, *flat, *near, *far[0], *far[1], b, g, lb)


def mlp_kernel(near, groups, bias_row, *refs):
    refs = list(refs)
    take = lambda n: [refs.pop(0) for _ in range(n)]
    norms = take(groups)
    bias_refs = take(2) if near else None
    n_arr = 2 if near else 8
    ups, downs = take(n_arr), take(n_arr)
    acc_in, res, bd_ref = (None, None, None) if near else (take(groups), take(groups), take(1)[0])
    (out,) = take(1)
    nb, rb, acc, ubuf, dbuf, bbuf, nsem, rsem, asem, usem, dsem, bsem = refs
    step = pl.program_id(0)
    n_steps = 4
    feats, width = ubuf.shape[2:]
    half = acc.shape[0] if acc.shape[0] <= MLP_ROWS else acc.shape[0] // 2

    def piece_copies(i, a):
        slot = i % 2
        if near:
            cols = slice(i * width, (i + 1) * width)
            up, down = ups[a].at[:, cols], downs[a].at[cols, :]
        else:
            up, down = ups[4 * a + i].at[:feats], downs[4 * a + i].at[:width]
        copies = [pltpu.make_async_copy(down, dbuf.at[slot, a * width:(a + 1) * width], dsem.at[slot, a]),
                  pltpu.make_async_copy(up, ubuf.at[slot, a], usem.at[slot, a])]
        if not near:
            copies.append(pltpu.make_async_copy(ups[4 * a + i].at[bias_row:bias_row + 16], bbuf.at[slot, a], bsem.at[slot, a]))
        return copies

    def rows_of(arrays, dst, sem):
        at, copies = 0, []
        for n, a in enumerate(arrays):
            copies.append(pltpu.make_async_copy(a, dst.at[at:at + a.shape[0]], sem.at[n]))
            at += a.shape[0]
        return copies

    def await_at(i, which):
        @pl.when(step == i)
        def _():
            for copy in which(i):
                copy.wait()

    @pl.when(step == 0)
    def _():
        for copy in rows_of(norms, nb, nsem) + [c for a in range(2) for c in piece_copies(0, a)]:
            copy.start()
        if near:
            acc[...] = jnp.zeros_like(acc)
        else:
            for copy in rows_of(acc_in, acc, asem) + rows_of(res, rb, rsem):
                copy.start()
        for copy in rows_of(norms, nb, nsem):
            copy.wait()

    for i in range(1, n_steps):
        @pl.when(step + 1 == i)
        def _(i=i):
            for copy in [c for a in range(2) for c in piece_copies(i, a)]:
                copy.start()

    slot = lax.rem(step, 2)
    for n in range(acc.shape[0] // half):
        rows = slice(n * half, (n + 1) * half)
        acts = []
        for a in range(2):
            if n == 0:
                for i in range(n_steps):
                    await_at(i, lambda i, a=a: piece_copies(i, a)[1:])
            bias = row_of(bias_refs[a], pl.ds(pl.multiple_of(step * width, width), width)) if near else bbuf[slot, a][:1, :].astype(F32)
            pre = jnp.dot(nb[rows, :], ubuf[slot, a], preferred_element_type=F32) + bias
            acts.append(jax.nn.gelu(pre, approximate=True).astype(BF16))
        if n == 0:
            for i in range(n_steps):
                await_at(i, lambda i: piece_copies(i, 0)[:1] + piece_copies(i, 1)[:1])
            if not near:
                await_at(0, lambda i: rows_of(acc_in, acc, asem))
        acc[rows, :] += jnp.dot(jnp.concatenate(acts, axis=1), dbuf[slot], preferred_element_type=F32)

    @pl.when(step == n_steps - 1)
    def _():
        if near:
            copy = pltpu.make_async_copy(acc, out, asem.at[0])
            copy.start()
            copy.wait()
        else:
            for copy in rows_of(res, rb, rsem):
                copy.wait()
            tok = out.shape[1]
            for n in range(out.shape[0]):
                rows = slice(n * tok, (n + 1) * tok)
                out[n] = (rb[rows, :].astype(F32) + acc[rows, :] + row_of(bd_ref)).astype(BF16)


def mlp(norms, bias, ups, downs, width, seqs, acc=None, res=None, bd=None, bias_row=None):
    feats = norms[0].shape[1]
    rows = sum(a.shape[0] for a in norms)
    whole = lambda a: pl.BlockSpec(a.shape, lambda n: (0,) * len(a.shape))
    hbm = pl.BlockSpec(memory_space=pl.ANY)
    near = acc is None
    if near:
        args = [*norms, *bias, *ups, *downs]
        specs = [hbm] * len(norms) + [whole(v) for v in bias] + [hbm] * (2 * len(ups))
        out_t, out_spec = jax.ShapeDtypeStruct((rows, feats), F32), hbm
    else:
        args = [*norms, *ups, *downs, *acc, *res, bd]
        specs = [hbm] * (len(args) - 1) + [whole(bd)]
        out_t = jax.ShapeDtypeStruct((seqs, rows // seqs, feats), BF16)
        out_spec = whole(out_t)
    return pl.pallas_call(
        functools.partial(mlp_kernel, near, len(norms), bias_row),
        grid=(4,),
        in_specs=specs, out_specs=out_spec, out_shape=out_t,
        scratch_shapes=[pltpu.VMEM((rows, feats), BF16), pltpu.VMEM((16 if near else rows, feats), BF16), pltpu.VMEM((rows, feats), F32), pltpu.VMEM((2, 2, feats, width), BF16),
                        pltpu.VMEM((2, 2 * width, feats), BF16), pltpu.VMEM((2, 2, 16, width), BF16), pltpu.SemaphoreType.DMA((len(norms),)), pltpu.SemaphoreType.DMA((len(norms),)),
                        pltpu.SemaphoreType.DMA((len(norms),)), pltpu.SemaphoreType.DMA((2, 2)), pltpu.SemaphoreType.DMA((2, 2)), pltpu.SemaphoreType.DMA((2, 2))],
        compiler_params=pltpu.CompilerParams(vmem_limit_bytes=VMEM_BIG),
        cost_estimate=pl.CostEstimate(flops=4 * rows * feats * 8 * width, bytes_accessed=4 * feats * 8 * width, transcendentals=0),
        name="mlp",
    )(*args)


def solution(mesh):
    tp_size, dp_size = mesh.shape['tp'], mesh.shape['dp']
    assert tp_size == 4 and dp_size == 4

    def tp_swap(a, k):
        return lax.ppermute(a, 'tp', [(i, i ^ k) for i in range(tp_size)])

    def dp_swap(a, k):
        return lax.ppermute(a, 'dp', [(i, i ^ k) for i in range(dp_size)])

    def local_layer(x_local, prefix_len, k_cache, v_cache, ln1_gain, ln1_bias, w_qkv, b_qkv, w_out, b_out, ln2_gain, ln2_bias, w_up, b_up, w_down, b_down):
        seqs, tok, feats = x_local.shape
        cache_len, heads, hd = k_cache.shape[1:]
        tp, dp = lax.axis_index('tp'), lax.axis_index('dp')
        idx = jnp.stack([tp, dp]).astype(jnp.int32)
        head_ids = tp * heads + jnp.arange(heads)
        slopes = jnp.exp2(-8.0 * (head_ids + 1).astype(F32) / (heads * tp_size))
        near_bias = [b_up, tp_swap(b_up, 1)]
        wo_s = tp_swap(w_out, 1)
        *normed, up_q, down_q = ln1(x_local, ln1_gain, ln1_bias, b_up, w_up, w_down, w_out, dp_size)
        x_x = [tp_swap(normed[b], 2) for b in range(seqs)]
        x_s = [tp_swap(normed[b], 1) for b in range(seqs)]
        x_xs = [tp_swap(x_x[b], 1) for b in range(seqs)]

        width = w_up.shape[1] // dp_size

        def spread(piece, a, b):
            first = tp_swap(piece, 2)
            one = dp_swap(first, a)
            two = dp_swap(first, b)
            both = dp_swap(one, b)
            got = [first, one, two, both] if a == 1 else [first, two, one, both]
            return got, [tp_swap(a, 1) for a in got]

        up_x, up_xs = spread(up_q, 1, 2)
        down_x, down_xs = spread(down_q, 2, 1)
        up_s, down_s = tp_swap(w_up, 1), tp_swap(w_down, 1)

        flat = (seqs, cache_len * heads, hd)
        ko, vo, kt, vt = prep(prefix_len, k_cache.reshape(flat), v_cache.reshape(flat), heads)
        ko, vo = ko.reshape(k_cache.shape), vo.reshape(v_cache.shape)
        got = []
        inter = (tok * tp_size, heads, hd)
        for b in range(seqs):
            q, kn, vn, ki, vi = qkv(idx, [normed[b], x_s[b], x_x[b], x_xs[b]], w_qkv, b_qkv, heads, hd)
            *ctx, ko, vo = attend(b, idx, prefix_len, slopes, q, kn, vn, kt, vt, ki.reshape(inter), vi.reshape(inter), ko, vo)
            got.append([ctx[0]] + [tp_swap(ctx[k], k) for k in (1, 2, 3)])
        norms, resid, acc = [], [], []
        for some in (tuple(range(seqs - 1)), (seqs - 1,)):
            r, n2 = out_proj(idx, x_local, some, [got[b] for b in some], [w_out, wo_s], [down_x, down_xs], width, b_out, ln2_gain, ln2_bias)
            resid.append(r)
            norms.append(n2)
            acc.append(mlp([n2], near_bias, [w_up, up_s], [w_down, down_s], width, seqs))
        out = mlp(norms, None, up_x + up_xs, down_x + down_xs, width, seqs, acc, resid, b_down, feats)
        return out, ko, vo

    tok_spec = P('dp', 'tp', None)
    cache_spec = P('dp', None, 'tp', None)
    rep = P()
    in_specs = (tok_spec, P('dp'), cache_spec, cache_spec, rep, rep, P(None, 'tp'), P('tp'), P('tp', None), rep, rep, rep, P(None, 'tp'), P('tp'), P('tp', None), rep)
    return jax.shard_map(local_layer, mesh=mesh, in_specs=in_specs, out_specs=(tok_spec, cache_spec, cache_spec), check_vma=False)
```

time: 1090 us -> 682 us (0.63)
  matrix products: 440 us -> 0 us
  Pallas kernels: 0 us -> 340 us
  other arithmetic: 121 us -> 1.18 us
  waiting for transfers between devices: 416 us -> 306 us
  local copies, waits for them, and re-layouts: 87.9 us -> 3.38 us
  starting transfers between devices: 0.69 us -> 21.7 us
  between operations: 14.5 us -> 1.22 us
    pallas_call x0 -> x15, Pallas kernels: none -> 340 us  [the longest x4 108 us: attend(): pl.pallas_call(functools.partial(attn_kernel, seq, heads), grid_spec=pltp...]
    ppermute x0 -> x44, waiting for transfers between devices: none -> 306 us  [the longest x6 171 us: dp_swap(): return lax.ppermute(a, 'dp', [(i, i ^ k) for i in range(dp_size)])]
    dot_general x5 -> x0, matrix products: 302 us -> none  [the longest x1 167 us: attend(): jnp.einsum('bhct,bthd->bchd', attn_probs, v_upd, preferred_element_type=j...]
    reduce_scatter x2 -> x0, waiting for transfers between devices: 240 us -> none  [the longest x1 120 us: local_layer(): lax.psum_scatter(attn_part, 'tp', scatter_dimension=1, tiled=True)]
    all_gather x2 -> x0, waiting for transfers between devices: 176 us -> none  [the longest x1 105 us: local_layer(): gathered2 = lax.all_gather(normed2, 'tp', axis=1, tiled=True)]
    sub x1 -> x0, matrix products: 138 us -> none  [attend(): attn_probs = jax.nn.softmax(scores, axis=-1).astype(jnp.bfloat16)]
    scatter x17 -> x0, other arithmetic: 61.7 us -> none
    scatter x32 -> x0, local copies, waits for them, and re-layouts: 37.5 us -> none
  transfers between devices with their start and end apart: 4 -> 44, of which waited for: 4 -> 16; matrix products, arithmetic and copies ran while one was open for 3% -> 0% of each run, Pallas kernels for 0% -> 42%
where the time goes in v1:
time: 682 us; the launch traced here: 673 us
  Pallas kernels  340 us (50%)
  waiting for transfers between devices  306 us (45%)
  starting transfers between devices  21.7 us (3%)
    ppermute x6, waiting for transfers between devices, dp_swap(): return lax.ppermute(a, 'dp', [(i, i ^ k) for i in range(dp_size)])  171 us
    ppermute x38, waiting for transfers between devices, tp_swap(): return lax.ppermute(a, 'tp', [(i, i ^ k) for i in range(tp_size)])  135 us
    pallas_call x4, Pallas kernels, attend(): pl.pallas_call(functools.partial(attn_kernel, seq, heads), grid_spec=pltp...  108 us
    pallas_call x3, Pallas kernels, mlp(): pl.pallas_call(functools.partial(mlp_kernel, near, len(norms), bias_row),...  105 us
    pallas_call x4, Pallas kernels, qkv(): pl.pallas_call(functools.partial(qkv_kernel, heads, hd, group), grid_spec...  55.8 us
    pallas_call x1, Pallas kernels, prep(): pl.pallas_call(functools.partial(prep_kernel, heads), grid_spec=pltpu.Pre...  33.2 us
    pallas_call x2, Pallas kernels, out_proj(): pl.pallas_call(functools.partial(out_kernel, seqs, far_row), grid_spec=pl...  28 us
    ppermute x38, starting transfers between devices, tp_swap(): return lax.ppermute(a, 'tp', [(i, i ^ k) for i in range(tp_size)])  17.1 us
  transfers between devices with their start and end apart: 44, of which 16 were waited for; matrix products, arithmetic and copies ran while one was open for 0% of the time, Pallas kernels for 42%

profile of v1, /device:TPU:0, one launch (start us, length us, event | category | flops | bytes accessed | tf_op | source)
XLA Modules:
  0.0 673.3 jit_solution(7690995731249389718)
XLA Ops:
  0.6 9.2 %ln1.1 = (bf16[256,2048]{1,0:T(8,128)(2,1)}, bf16[256,2048]{1,0:T(8,128)(2,1)}, bf16[256,2048]{1,0:T(8,128)(2,1)}, bf16[256,2048]{1,0:T(8,128)(2,1)}, bf16[2064,...) custom-call(bf16[4,256,2048]{2,1,0:T(8,128)(2,1)} %refs_1_.5, bf16[2048]{0:T(1024)(128)(2,1)} %g_ref.1, ...), custom_call_target="tpu_custom_call" | custom-call | flops 2000000000 | bytes 16777216 | tf_op jit(solution)/shard_map/ln1/pallas_call | solution.py:116
  9.8 3.2 collective-permute-start.1
  13.1 0.1 collective-permute-start.7
  13.1 0.4 collective-permute-start.6
  13.6 1.7 collective-permute-start.13
  15.3 0.5 multiply_exponential_fusion.slope_ref
  15.8 0.6 pad_add_fusion.idx_ref.refs_0_
  16.5 20.8 %collective-permute-done.1.p2 = bf16[256,2048]{1,0:T(8,128)(2,1)S(1)} collective-permute-done((bf16[256,2048]{1,0:T(8,128)(2,1)}, bf16[256,2048]{1,0:T(8,128)(2,1)S(1)}, u32[]{:S(2)}, u32[]{:S(2)}) %collective-permute-start.1) | collective-permute-done | bytes 1048608 | tf_op jit(solution)/shard_map/ppermute | solution.py:508
  37.3 33.2 %prep.1 = (bf16[4,16384,128]{2,1,0:T(8,128)(2,1)}, bf16[4,16384,128]{2,1,0:T(8,128)(2,1)}, bf16[4,4,4096,128]{3,2,1,0:T(8,128)(2,1)}, bf16[4,4,4096,128]{3,2,1,0:T(8,128)(2,1)}) custom-call(s32[4]{0:T(128)} %len_ref.9, bf16[4,16384,128]{2,1,0:T(8,128)(2,1)} %bitcast.24, bf16[4,16384,128]{2,1,0:T(8,128)(2,1)} %bitcast.25), custom_call_target="tpu_custom_call" | custom-call | flops 20000000000 | bytes 100663296 | tf_op jit(solution)/shard_map/prep/pallas_call | solution.py:53
  70.4 0.5 collective-permute-start.12
  71.0 2.0 collective-permute-start.28
  73.0 13.9 %qkv.4 = (bf16[4,1024,128]{2,1,0:T(8,128)(2,1)}, bf16[4,1024,128]{2,1,0:T(8,128)(2,1)}, bf16[4,1024,128]{2,1,0:T(8,128)(2,1)}, bf16[4096,128]{1,0:T(8,128)(2,1)}, bf16[4096,128]{1,0:T(8,128)(2,1)}) custom-call(s32[2]{0:T(128)} %pad_add_fusion.idx_ref.refs_0_, bf16[256,2048]{1,0:T(8,128)(2,1)} %get-tuple-element.61.p0, ...), custom_call_target="tpu_custom_call" | custom-call | flops 6442450944 | bytes 10485760 | tf_op jit(solution)/shard_map/qkv/pallas_call | solution.py:176
  87.0 28.1 %attend.4 = (bf16[256,512]{1,0:T(8,128)(2,1)}, bf16[256,512]{1,0:T(8,128)(2,1)}, bf16[256,512]{1,0:T(8,128)(2,1)}, bf16[256,512]{1,0:T(8,128)(2,1)}, bf16[4,4096...) custom-call(s32[2]{0:T(128)} %pad_add_fusion.idx_ref.refs_0_, ...), custom_call_target="tpu_custom_call", output_to_operand_aliasing={{4}: (10, {}), {5}: (11, {})} | custom-call | flops 10737418240 | bytes 8388608 | tf_op jit(solution)/shard_map/attend/pallas_call | solution.py:304
  115.1 0.5 collective-permute-start.27
  115.7 0.4 collective-permute-start.14
  116.2 14.0 %qkv.5 = (bf16[4,1024,128]{2,1,0:T(8,128)(2,1)}, bf16[4,1024,128]{2,1,0:T(8,128)(2,1)}, bf16[4,1024,128]{2,1,0:T(8,128)(2,1)}, bf16[4096,128]{1,0:T(8,128)(2,1)}, bf16[4096,128]{1,0:T(8,128)(2,1)}) custom-call(s32[2]{0:T(128)} %pad_add_fusion.idx_ref.refs_0_, bf16[256,2048]{1,0:T(8,128)(2,1)} %get-tuple-element.75.p0, ...), custom_call_target="tpu_custom_call" | custom-call | flops 6442450944 | bytes 10485760 | tf_op jit(solution)/shard_map/qkv/pallas_call | solution.py:176
  130.2 28.2 %attend.5 = (bf16[256,512]{1,0:T(8,128)(2,1)}, bf16[256,512]{1,0:T(8,128)(2,1)}, bf16[256,512]{1,0:T(8,128)(2,1)}, bf16[256,512]{1,0:T(8,128)(2,1)}, bf16[4,4096...) custom-call(s32[2]{0:T(128)} %pad_add_fusion.idx_ref.refs_0_, ...), custom_call_target="tpu_custom_call", output_to_operand_aliasing={{4}: (10, {}), {5}: (11, {})} | custom-call | flops 10737418240 | bytes 8388608 | tf_op jit(solution)/shard_map/attend/pallas_call | solution.py:304
  158.4 0.1 collective-permute-start.19
  158.5 2.0 collective-permute-start.33
  160.5 14.0 %qkv.6 = (bf16[4,1024,128]{2,1,0:T(8,128)(2,1)}, bf16[4,1024,128]{2,1,0:T(8,128)(2,1)}, bf16[4,1024,128]{2,1,0:T(8,128)(2,1)}, bf16[4096,128]{1,0:T(8,128)(2,1)}, bf16[4096,128]{1,0:T(8,128)(2,1)}) custom-call(s32[2]{0:T(128)} %pad_add_fusion.idx_ref.refs_0_, bf16[256,2048]{1,0:T(8,128)(2,1)} %get-tuple-element.87.p0, ...), custom_call_target="tpu_custom_call" | custom-call | flops 6442450944 | bytes 10485760 | tf_op jit(solution)/shard_map/qkv/pallas_call | solution.py:176
  174.4 14.0 %qkv.7 = (bf16[4,1024,128]{2,1,0:T(8,128)(2,1)}, bf16[4,1024,128]{2,1,0:T(8,128)(2,1)}, bf16[4,1024,128]{2,1,0:T(8,128)(2,1)}, bf16[4096,128]{1,0:T(8,128)(2,1)}, bf16[4096,128]{1,0:T(8,128)(2,1)}) custom-call(s32[2]{0:T(128)} %pad_add_fusion.idx_ref.refs_0_, bf16[256,2048]{1,0:T(8,128)(2,1)} %get-tuple-element.101.p0, ...), custom_call_target="tpu_custom_call" | custom-call | flops 6442450944 | bytes 10485760 | tf_op jit(solution)/shard_map/qkv/pallas_call | solution.py:176
  188.4 20.8 %attend.6 = (bf16[256,512]{1,0:T(8,128)(2,1)}, bf16[256,512]{1,0:T(8,128)(2,1)}, bf16[256,512]{1,0:T(8,128)(2,1)}, bf16[256,512]{1,0:T(8,128)(2,1)}, bf16[4,4096...) custom-call(s32[2]{0:T(128)} %pad_add_fusion.idx_ref.refs_0_, ...), custom_call_target="tpu_custom_call", output_to_operand_aliasing={{4}: (10, {}), {5}: (11, {})} | custom-call | flops 10737418240 | bytes 8388608 | tf_op jit(solution)/shard_map/attend/pallas_call | solution.py:304
  209.2 54.0 %collective-permute-done.33.refs_2_ = bf16[2064,512]{1,0:T(8,128)(2,1)} collective-permute-done((bf16[2064,512]{1,0:T(8,128)(2,1)}, bf16[2064,512]{1,0:T(8,128)(2,1)}, u32[]{:S(2)}, u32[]{:S(2)}) %collective-permute-start.33) | collective-permute-done | bytes 2113568 | tf_op jit(solution)/shard_map/ppermute | solution.py:508
  263.3 31.3 %attend.7 = (bf16[256,512]{1,0:T(8,128)(2,1)}, bf16[256,512]{1,0:T(8,128)(2,1)}, bf16[256,512]{1,0:T(8,128)(2,1)}, bf16[256,512]{1,0:T(8,128)(2,1)}, bf16[4,4096...) custom-call(s32[2]{0:T(128)} %pad_add_fusion.idx_ref.refs_0_, ...), custom_call_target="tpu_custom_call", output_to_operand_aliasing={{4}: (10, {}), {5}: (11, {})} | custom-call | flops 10737418240 | bytes 8388608 | tf_op jit(solution)/shard_map/attend/pallas_call | solution.py:304
  294.7 0.5 collective-permute-start.41
  295.1 1.2 collective-permute-done.41.refs_2_
  296.4 0.1 collective-permute-start.42
  296.5 0.4 collective-permute-start.43
  296.9 0.3 collective-permute-start.31
  297.2 1.1 collective-permute-start.21
  298.3 7.2 %collective-permute-done.31.refs_4_ = bf16[256,512]{1,0:T(8,128)(2,1)S(1)} collective-permute-done((bf16[256,512]{1,0:T(8,128)(2,1)}, bf16[256,512]{1,0:T(8,128)(2,1)S(1)}, u32[]{:S(2)}, u32[]{:S(2)}) %collective-permute-start.31) | collective-permute-done | bytes 262176 | tf_op jit(solution)/shard_map/ppermute | solution.py:508
  305.5 8.4 %collective-permute-done.32.refs_5_ = bf16[256,512]{1,0:T(8,128)(2,1)S(1)} collective-permute-done((bf16[256,512]{1,0:T(8,128)(2,1)}, bf16[256,512]{1,0:T(8,128)(2,1)S(1)}, u32[]{:S(2)}, u32[]{:S(2)}) %collective-permute-start.32) | collective-permute-done | bytes 262176 | tf_op jit(solution)/shard_map/ppermute | solution.py:508
  313.9 8.3 %collective-permute-done.15.refs_11_ = bf16[256,512]{1,0:T(8,128)(2,1)S(1)} collective-permute-done((bf16[256,512]{1,0:T(8,128)(2,1)}, bf16[256,512]{1,0:T(8,128)(2,1)S(1)}, u32[]{:S(2)}, u32[]{:S(2)}) %collective-permute-start.15) | collective-permute-done | bytes 262176 | tf_op jit(solution)/shard_map/ppermute | solution.py:508
  322.1 0.3 collective-permute-start.16
  322.4 8.1 %collective-permute-done.16.refs_12_ = bf16[256,512]{1,0:T(8,128)(2,1)S(1)} collective-permute-done((bf16[256,512]{1,0:T(8,128)(2,1)S(1)}, bf16[256,512]{1,0:T(8,128)(2,1)S(1)}, u32[]{:S(2)}, u32[]{:S(2)}) %collective-permute-start.16) | collective-permute-done | bytes 262176 | tf_op jit(solution)/shard_map/ppermute | solution.py:508
  330.5 8.1 %collective-permute-done.17.refs_13_ = bf16[256,512]{1,0:T(8,128)(2,1)S(1)} collective-permute-done((bf16[256,512]{1,0:T(8,128)(2,1)S(1)}, bf16[256,512]{1,0:T(8,128)(2,1)S(1)}, u32[]{:S(2)}, u32[]{:S(2)}) %collective-permute-start.17) | collective-permute-done | bytes 262176 | tf_op jit(solution)/shard_map/ppermute | solution.py:508
  338.6 0.5 collective-permute-start.10
  339.1 7.5 %collective-permute-done.10.refs_8_ = bf16[256,512]{1,0:T(8,128)(2,1)S(1)} collective-permute-done((bf16[256,512]{1,0:T(8,128)(2,1)}, bf16[256,512]{1,0:T(8,128)(2,1)S(1)}, u32[]{:S(2)}, u32[]{:S(2)}) %collective-permute-start.10) | collective-permute-done | bytes 262176 | tf_op jit(solution)/shard_map/ppermute | solution.py:508
  346.6 0.5 collective-permute-start.11
  347.1 8.3 %collective-permute-done.11.refs_9_ = bf16[256,512]{1,0:T(8,128)(2,1)} collective-permute-done((bf16[256,512]{1,0:T(8,128)(2,1)}, bf16[256,512]{1,0:T(8,128)(2,1)}, u32[]{:S(2)}, u32[]{:S(2)}) %collective-permute-start.11) | collective-permute-done | bytes 262176 | tf_op jit(solution)/shard_map/ppermute | solution.py:508
  355.5 0.6 collective-permute-done.21.refs_18_.refs_10_.refs_12_
  356.1 1.4 collective-permute-start.22
  357.5 57.9 %collective-permute-done.20.refs_17_.refs_9_.refs_11_ = bf16[640,2048]{1,0:T(8,128)(2,1)S(1)} collective-permute-done((bf16[640,2048]{1,0:T(8,128)(2,1)}, bf16[640,2048]{1,0:T(8,128)(2,1)S(1)}, u32[]{:S(2)}, u32[]{:S(2)}) %collective-permute-start.20) | collective-permute-done | bytes 2621472 | tf_op jit(solution)/shard_map/ppermute | solution.py:511
  415.4 0.5 collective-permute-start.24
  415.9 54.7 %collective-permute-done.22.refs_19_.refs_11_.refs_13_ = bf16[640,2048]{1,0:T(8,128)(2,1)S(1)} collective-permute-done((bf16[640,2048]{1,0:T(8,128)(2,1)S(1)}, bf16[640,2048]{1,0:T(8,128)(2,1)S(1)}, u32[]{:S(2)}, u32[]{:S(2)}) %collective-permute-start.22) | collective-permute-done | bytes 2621472 | tf_op jit(solution)/shard_map/ppermute | solution.py:511
  470.6 0.9 collective-permute-start.35
  471.6 1.2 collective-permute-start.36
  472.8 2.8 collective-permute-done.26.refs_23_.refs_15_.refs_17_
  475.5 0.1 collective-permute-start.9
  475.7 1.3 copy-done.7
  477.0 9.7 %outp.3 = (bf16[256,2048]{1,0:T(8,128)(2,1)}, bf16[256,2048]{1,0:T(8,128)(2,1)}) custom-call(s32[2]{0:T(128)} %pad_add_fusion.idx_ref.refs_0_, bf16[4,256,2048]{2,1,0:T(8,128)(2,1)} %refs_1_.5, bf16[256,512]{1,0:T(8,128)(2,1)} %get-tuple-element.109.refs_2_, bf16[256,512]{1,0:T(8,128)(2,1)} %copy-done.11, bf16[256,512]{1,0:T(8,128)(2,1)} %copy-done.13, ...), custom_call_target="tpu_custom_call" | custom-call | flops 2147483648 | bytes 8388608 | tf_op jit(solution)/shard_map/outp/pallas_call | solution.py:368
  486.8 0.2 collective-permute-start.3
  487.0 1.0 collective-permute-start.4
  488.0 0.7 collective-permute-start.5
  488.7 17.1 %mlp.4.refs_19_ = f32[256,2048]{1,0:T(8,128)} custom-call(bf16[256,2048]{1,0:T(8,128)(2,1)} %get-tuple-element.113.refs_0_.refs_1_, bf16[2048]{0:T(1024)(128)(2,1)} %refs_1_.7, bf16[2048]{0:T(1024)(128)(2,1)} %copy-done.19, bf16[2048,2048]{1,0:T(8,128)(2,1)} %refs_3_.3, bf16[2048,2048]{1,0:T(8,128)(2,1)} %collective-permute-done.42.refs_4_, ...), custom_call_target="tpu_custom_call" | custom-call | flops 8589934592 | bytes 33554432 | tf_op jit(solution)/shard_map/mlp/pallas_call | solution.py:490
  505.9 0.5 collective-permute-start.37
  506.3 0.1 collective-permute-start.38
  506.4 13.4 %collective-permute-done.35.refs_4_ = bf16[2064,512]{1,0:T(8,128)(2,1)} collective-permute-done((bf16[2064,512]{1,0:T(8,128)(2,1)}, bf16[2064,512]{1,0:T(8,128)(2,1)}, u32[]{:S(2)}, u32[]{:S(2)}) %collective-permute-start.35) | collective-permute-done | bytes 2113568 | tf_op jit(solution)/shard_map/ppermute | solution.py:511
  519.9 44.8 %collective-permute-done.36.refs_5_ = bf16[2064,512]{1,0:T(8,128)(2,1)} collective-permute-done((bf16[2064,512]{1,0:T(8,128)(2,1)}, bf16[2064,512]{1,0:T(8,128)(2,1)}, u32[]{:S(2)}, u32[]{:S(2)}) %collective-permute-start.36) | collective-permute-done | bytes 2113568 | tf_op jit(solution)/shard_map/ppermute | solution.py:511
  564.7 0.7 copy-done.17
  565.4 18.3 %outp.2 = (bf16[768,2048]{1,0:T(8,128)(2,1)}, bf16[768,2048]{1,0:T(8,128)(2,1)}) custom-call(s32[2]{0:T(128)} %pad_add_fusion.idx_ref.refs_0_, bf16[4,256,2048]{2,1,0:T(8,128)(2,1)} %refs_1_.5, bf16[256,512]{1,0:T(8,128)(2,1)} %get-tuple-element.71.refs_2_, bf16[256,512]{1,0:T(8,128)(2,1)} %copy-done.15, bf16[256,512]{1,0:T(8,128)(2,1)} %copy-done.16, ...), custom_call_target="tpu_custom_call" | custom-call | flops 6442450944 | bytes 8388608 | tf_op jit(solution)/shard_map/outp/pallas_call | solution.py:368
  583.7 37.7 %mlp.3.refs_18_ = f32[768,2048]{1,0:T(8,128)} custom-call(bf16[768,2048]{1,0:T(8,128)(2,1)} %get-tuple-element.100.refs_0_, bf16[2048]{0:T(1024)(128)(2,1)} %refs_1_.7, bf16[2048]{0:T(1024)(128)(2,1)} %copy-done.19, bf16[2048,2048]{1,0:T(8,128)(2,1)} %refs_3_.3, bf16[2048,2048]{1,0:T(8,128)(2,1)} %collective-permute-done.42.refs_4_, ...), custom_call_target="tpu_custom_call" | custom-call | flops 25769803776 | bytes 33554432 | tf_op jit(solution)/shard_map/mlp/pallas_call | solution.py:490
  621.4 1.3 copy-done.20
  622.7 50.4 %mlp.5 = bf16[4,256,2048]{2,1,0:T(8,128)(2,1)} custom-call(bf16[768,2048]{1,0:T(8,128)(2,1)} %get-tuple-element.100.refs_0_, bf16[256,2048]{1,0:T(8,128)(2,1)} %get-tuple-element.113.refs_0_.refs_1_, bf16[2064,512]{1,0:T(8,128)(2,1)} %collective-permute-done.33.refs_2_, bf16[2064,512]{1,0:T(8,128)(2,1)} %collective-permute-done.34.refs_3_, ...), custom_call_target="tpu_custom_call" | custom-call | flops 34359738368 | bytes 33554432 | tf_op jit(solution)/shard_map/mlp/pallas_call | solution.py:490
  (91 shorter events, 0.4 us)
Async XLA Ops:
  9.8 27.4 %collective-permute-start.1 = (bf16[256,2048]{1,0:T(8,128)(2,1)}, bf16[256,2048]{1,0:T(8,128)(2,1)S(1)}, u32[]{:S(2)}, u32[]{:S(2)}) collective-permute-start(bf16[256,2048]{1,0:T(8,128)(2,1)} %get-tuple-element.61.p0), channel_id=1, source_target_pairs={{0,2},{1,3},{2,0},{3,1},{4,6},{5,7},{6,4},{7,5},{8,10},{9,11},{10,... | collective-permute-start | bytes 3145736 | tf_op jit(solution)/shard_map/ppermute | solution.py:508
  13.0 57.4 %collective-permute-start = (bf16[256,2048]{1,0:T(8,128)(2,1)}, bf16[256,2048]{1,0:T(8,128)(2,1)}, u32[]{:S(2)}, u32[]{:S(2)}) collective-permute-start(bf16[256,2048]{1,0:T(8,128)(2,1)} %get-tuple-element.61.p0), channel_id=1, source_target_pairs={{0,1},{1,0},{2,3},{3,2},{4,5},{5,4},{6,7},{7,6},{8,9},{9,8},{10,11... | collective-permute-start | bytes 3145736 | tf_op jit(solution)/shard_map/ppermute | solution.py:508
  13.1 57.9 %collective-permute-start.7 = (bf16[256,2048]{1,0:T(8,128)(2,1)}, bf16[256,2048]{1,0:T(8,128)(2,1)}, u32[]{:S(2)}, u32[]{:S(2)}) collective-permute-start(bf16[256,2048]{1,0:T(8,128)(2,1)} %get-tuple-element.75.p0), channel_id=1, source_target_pairs={{0,2},{1,3},{2,0},{3,1},{4,6},{5,7},{6,4},{7,5},{8,10},{9,11},{10,... | collective-permute-start | bytes 3145736 | tf_op jit(solution)/shard_map/ppermute | solution.py:508
  13.1 102.0 %collective-permute-start.6 = (bf16[256,2048]{1,0:T(8,128)(2,1)}, bf16[256,2048]{1,0:T(8,128)(2,1)}, u32[]{:S(2)}, u32[]{:S(2)}) collective-permute-start(bf16[256,2048]{1,0:T(8,128)(2,1)} %get-tuple-element.75.p0), channel_id=1, source_target_pairs={{0,1},{1,0},{2,3},{3,2},{4,5},{5,4},{6,7},{7,6},{8,9},{9,8},{10,11... | collective-permute-start | bytes 3145736 | tf_op jit(solution)/shard_map/ppermute | solution.py:508
  13.6 102.1 %collective-permute-start.13 = (bf16[256,2048]{1,0:T(8,128)(2,1)}, bf16[256,2048]{1,0:T(8,128)(2,1)}, u32[]{:S(2)}, u32[]{:S(2)}) collective-permute-start(bf16[256,2048]{1,0:T(8,128)(2,1)} %get-tuple-element.87.p0), channel_id=1, source_target_pairs={{0,2},{1,3},{2,0},{3,1},{4,6},{5,7},{6,4},{7,5},{8,10},{9,11},{10,... | collective-permute-start | bytes 3145736 | tf_op jit(solution)/shard_map/ppermute | solution.py:508
  37.3 33.2 %copy-start.22 = (bf16[256,2048]{1,0:T(8,128)(2,1)}, bf16[256,2048]{1,0:T(8,128)(2,1)S(1)}, u32[]{:S(2)}) copy-start(bf16[256,2048]{1,0:T(8,128)(2,1)S(1)} %collective-permute-done.1.p2) | copy-start | bytes 3145732
  37.3 35.7 %collective-permute-start.2 = (bf16[256,2048]{1,0:T(8,128)(2,1)S(1)}, bf16[256,2048]{1,0:T(8,128)(2,1)}, u32[]{:S(2)}, u32[]{:S(2)}) collective-permute-start(bf16[256,2048]{1,0:T(8,128)(2,1)S(1)} %collective-permute-done.1.p2), channel_id=1, source_target_pairs={{0,1},{1,0},{2,3},{3,2},{4,5},{5,4},{6,7},{7,6},{8,9},{9,8},{10,11... | collective-permute-start | bytes 3145736 | tf_op jit(solution)/shard_map/ppermute | solution.py:508
  37.3 33.7 %copy-start.21 = (bf16[256,2048]{1,0:T(8,128)(2,1)S(1)}, bf16[256,2048]{1,0:T(8,128)(2,1)}, u32[]{:S(2)}) copy-start(bf16[256,2048]{1,0:T(8,128)(2,1)} %get-tuple-element.101.p0) | copy-start | bytes 3145732
  70.4 87.9 %collective-permute-start.12 = (bf16[256,2048]{1,0:T(8,128)(2,1)}, bf16[256,2048]{1,0:T(8,128)(2,1)}, u32[]{:S(2)}, u32[]{:S(2)}) collective-permute-start(bf16[256,2048]{1,0:T(8,128)(2,1)} %get-tuple-element.87.p0), channel_id=1, source_target_pairs={{0,1},{1,0},{2,3},{3,2},{4,5},{5,4},{6,7},{7,6},{8,9},{9,8},{10,11... | collective-permute-start | bytes 3145736 | tf_op jit(solution)/shard_map/ppermute | solution.py:508
  71.0 44.7 %collective-permute-start.28 = (bf16[256,2048]{1,0:T(8,128)(2,1)S(1)}, bf16[256,2048]{1,0:T(8,128)(2,1)}, u32[]{:S(2)}, u32[]{:S(2)}) collective-permute-start(bf16[256,2048]{1,0:T(8,128)(2,1)S(1)} %copy-done.21), channel_id=1, source_target_pairs={{0,2},{1,3},{2,0},{3,1},{4,6},{5,7},{6,4},{7,5},{8,10},{9,11},{10,... | collective-permute-start | bytes 3145736 | tf_op jit(solution)/shard_map/ppermute | solution.py:508
  73.0 43.2 %collective-permute-start.8 = (bf16[256,2048]{1,0:T(8,128)(2,1)}, bf16[256,2048]{1,0:T(8,128)(2,1)}, u32[]{:S(2)}, u32[]{:S(2)}) collective-permute-start(bf16[256,2048]{1,0:T(8,128)(2,1)} %collective-permute-done.7.p2), channel_id=1, source_target_pairs={{0,1},{1,0},{2,3},{3,2},{4,5},{5,4},{6,7},{7,6},{8,9},{9,8},{10,11... | collective-permute-start | bytes 3145736 | tf_op jit(solution)/shard_map/ppermute | solution.py:508
  87.0 28.7 %copy-start = (bf16[512,2048]{1,0:T(8,128)(2,1)S(1)}, bf16[512,2048]{1,0:T(8,128)(2,1)}, u32[]{:S(2)}) copy-start(bf16[512,2048]{1,0:T(8,128)(2,1)} %refs_6_.1) | copy-start | bytes 6291460
  115.1 59.3 %collective-permute-start.27 = (bf16[256,2048]{1,0:T(8,128)(2,1)S(1)}, bf16[256,2048]{1,0:T(8,128)(2,1)}, u32[]{:S(2)}, u32[]{:S(2)}) collective-permute-start(bf16[256,2048]{1,0:T(8,128)(2,1)S(1)} %copy-done.21), channel_id=1, source_target_pairs={{0,1},{1,0},{2,3},{3,2},{4,5},{5,4},{6,7},{7,6},{8,9},{9,8},{10,11... | collective-permute-start | bytes 3145736 | tf_op jit(solution)/shard_map/ppermute | solution.py:508
  115.7 180.9 %collective-permute-start.18 = (bf16[512,2048]{1,0:T(8,128)(2,1)S(1)}, bf16[512,2048]{1,0:T(8,128)(2,1)}, u32[]{:S(2)}, u32[]{:S(2)}) collective-permute-start(bf16[512,2048]{1,0:T(8,128)(2,1)S(1)} %copy-done), channel_id=1, source_target_pairs={{0,1},{1,0},{2,3},{3,2},{4,5},{5,4},{6,7},{7,6},{8,9},{9,8},{10,11... | collective-permute-start | bytes 6291464 | tf_op jit(solution)/shard_map/ppermute | solution.py:508
  115.7 42.7 %collective-permute-start.14 = (bf16[256,2048]{1,0:T(8,128)(2,1)}, bf16[256,2048]{1,0:T(8,128)(2,1)}, u32[]{:S(2)}, u32[]{:S(2)}) collective-permute-start(bf16[256,2048]{1,0:T(8,128)(2,1)} %collective-permute-done.13.p2), channel_id=1, source_target_pairs={{0,1},{1,0},{2,3},{3,2},{4,5},{5,4},{6,7},{7,6},{8,9},{9,8},{10,11... | collective-permute-start | bytes 3145736 | tf_op jit(solution)/shard_map/ppermute | solution.py:508
  116.2 58.3 %collective-permute-start.29 = (bf16[256,2048]{1,0:T(8,128)(2,1)}, bf16[256,2048]{1,0:T(8,128)(2,1)}, u32[]{:S(2)}, u32[]{:S(2)}) collective-permute-start(bf16[256,2048]{1,0:T(8,128)(2,1)} %collective-permute-done.28.p2), channel_id=1, source_target_pairs={{0,1},{1,0},{2,3},{3,2},{4,5},{5,4},{6,7},{7,6},{8,9},{9,8},{10,11... | collective-permute-start | bytes 3145736 | tf_op jit(solution)/shard_map/ppermute | solution.py:508
  158.4 138.8 %collective-permute-start.19 = (bf16[640,2048]{1,0:T(8,128)(2,1)}, bf16[640,2048]{1,0:T(8,128)(2,1)}, u32[]{:S(2)}, u32[]{:S(2)}) collective-permute-start(bf16[640,2048]{1,0:T(8,128)(2,1)} %get-tuple-element.99), channel_id=1, source_target_pairs={{0,2},{1,3},{2,0},{3,1},{4,6},{5,7},{6,4},{7,5},{8,10},{9,11},{10,... | collective-permute-start | bytes 7864328 | tf_op jit(solution)/shard_map/ppermute | solution.py:508
  158.5 104.8 %collective-permute-start.33 = (bf16[2064,512]{1,0:T(8,128)(2,1)}, bf16[2064,512]{1,0:T(8,128)(2,1)}, u32[]{:S(2)}, u32[]{:S(2)}) collective-permute-start(bf16[2064,512]{1,0:T(8,128)(2,1)} %get-tuple-element.114), channel_id=1, source_target_pairs={{0,2},{1,3},{2,0},{3,1},{4,6},{5,7},{6,4},{7,5},{8,10},{9,11},{10,... | collective-permute-start | bytes 6340616 | tf_op jit(solution)/shard_map/ppermute | solution.py:508
  263.2 92.2 %collective-permute-start.34 = (bf16[2064,512]{1,0:T(8,128)(2,1)}, bf16[2064,512]{1,0:T(8,128)(2,1)}, u32[]{:S(2)}, u32[]{:S(2)}) collective-permute-start(bf16[2064,512]{1,0:T(8,128)(2,1)} %collective-permute-done.33.refs_2_), channel_id=1, source_target_pairs={{0,4},{4,0},{8,12},{12,8},{1,5},{5,1},{9,13},{13,9},{2,6},{6,2},{1... | collective-permute-start | bytes 6340616 | tf_op jit(solution)/shard_map/ppermute | solution.py:511
  263.2 31.4 %copy-start.18 = (bf16[2048]{0:T(1024)(128)(2,1)S(1)}, bf16[2048]{0:T(1024)(128)(2,1)}, u32[]{:S(2)}) copy-start(bf16[2048]{0:T(1024)(128)(2,1)} %refs_1_.7) | copy-start | bytes 12292
  263.2 58.9 %copy-start.24 = (bf16[256,512]{1,0:T(8,128)(2,1)S(1)}, bf16[256,512]{1,0:T(8,128)(2,1)}, u32[]{:S(2)}) copy-start(bf16[256,512]{1,0:T(8,128)(2,1)} %get-tuple-element.97) | copy-start | bytes 786436
  263.3 67.3 %copy-start.23 = (bf16[256,512]{1,0:T(8,128)(2,1)S(1)}, bf16[256,512]{1,0:T(8,128)(2,1)}, u32[]{:S(2)}) copy-start(bf16[256,512]{1,0:T(8,128)(2,1)} %get-tuple-element.98) | copy-start | bytes 786436
  294.6 2.3 collective-permute-start.30
  294.7 1.7 collective-permute-start.41
  296.4 190.4 %copy-start.19 = (bf16[2048]{0:T(1024)(128)(2,1)}, bf16[2048]{0:T(1024)(128)(2,1)S(1)}, u32[]{:S(2)}) copy-start(bf16[2048]{0:T(1024)(128)(2,1)S(1)} %collective-permute-done.41.refs_2_) | copy-start | bytes 12292
  296.4 190.6 %collective-permute-start.42 = (bf16[2048,2048]{1,0:T(8,128)(2,1)}, bf16[2048,2048]{1,0:T(8,128)(2,1)}, u32[]{:S(2)}, u32[]{:S(2)}) collective-permute-start(bf16[2048,2048]{1,0:T(8,128)(2,1)} %refs_3_.3), channel_id=1, source_target_pairs={{0,1},{1,0},{2,3},{3,2},{4,5},{5,4},{6,7},{7,6},{8,9},{9,8},{10,11... | collective-permute-start | bytes 25165832 | tf_op jit(solution)/shard_map/ppermute | solution.py:508
  296.5 191.5 %collective-permute-start.43 = (bf16[2048,2048]{1,0:T(8,128)(2,1)}, bf16[2048,2048]{1,0:T(8,128)(2,1)}, u32[]{:S(2)}, u32[]{:S(2)}) collective-permute-start(bf16[2048,2048]{1,0:T(8,128)(2,1)} %refs_5_.3), channel_id=1, source_target_pairs={{0,1},{1,0},{2,3},{3,2},{4,5},{5,4},{6,7},{7,6},{8,9},{9,8},{10,11... | collective-permute-start | bytes 25165832 | tf_op jit(solution)/shard_map/ppermute | solution.py:508
  296.9 180.1 %copy-start.11 = (bf16[256,512]{1,0:T(8,128)(2,1)}, bf16[256,512]{1,0:T(8,128)(2,1)S(1)}, u32[]{:S(2)}) copy-start(bf16[256,512]{1,0:T(8,128)(2,1)S(1)} %collective-permute-done.30.refs_3_) | copy-start | bytes 786436
  296.9 8.6 %collective-permute-start.31 = (bf16[256,512]{1,0:T(8,128)(2,1)}, bf16[256,512]{1,0:T(8,128)(2,1)S(1)}, u32[]{:S(2)}, u32[]{:S(2)}) collective-permute-start(bf16[256,512]{1,0:T(8,128)(2,1)} %get-tuple-element.111), channel_id=1, source_target_pairs={{0,2},{1,3},{2,0},{3,1},{4,6},{5,7},{6,4},{7,5},{8,10},{9,11},{10,... | collective-permute-start | bytes 786440 | tf_op jit(solution)/shard_map/ppermute | solution.py:508
  297.2 58.9 %collective-permute-start.21 = (bf16[640,2048]{1,0:T(8,128)(2,1)}, bf16[640,2048]{1,0:T(8,128)(2,1)S(1)}, u32[]{:S(2)}, u32[]{:S(2)}) collective-permute-start(bf16[640,2048]{1,0:T(8,128)(2,1)} %collective-permute-done.19.refs_16_.refs_8_.refs_10_), channel_id=1, source_target_pairs={{0,8},{4,12},{8,0},{12,4},{1,9},{5,13},{9,1},{13,5},{2,10},{6,14},... | collective-permute-start | bytes 7864328 | tf_op jit(solution)/shard_map/ppermute | solution.py:511
  305.5 8.4 %copy-start.13 = (bf16[256,512]{1,0:T(8,128)(2,1)}, bf16[256,512]{1,0:T(8,128)(2,1)S(1)}, u32[]{:S(2)}) copy-start(bf16[256,512]{1,0:T(8,128)(2,1)S(1)} %collective-permute-done.31.refs_4_) | copy-start | bytes 786436
  305.5 8.4 %collective-permute-start.32 = (bf16[256,512]{1,0:T(8,128)(2,1)}, bf16[256,512]{1,0:T(8,128)(2,1)S(1)}, u32[]{:S(2)}, u32[]{:S(2)}) collective-permute-start(bf16[256,512]{1,0:T(8,128)(2,1)} %get-tuple-element.112), channel_id=1, source_target_pairs={{0,3},{1,2},{2,1},{3,0},{4,7},{5,6},{6,5},{7,4},{8,11},{9,10},{10,... | collective-permute-start | bytes 786440 | tf_op jit(solution)/shard_map/ppermute | solution.py:508
  313.9 8.3 %copy-start.14 = (bf16[256,512]{1,0:T(8,128)(2,1)}, bf16[256,512]{1,0:T(8,128)(2,1)S(1)}, u32[]{:S(2)}) copy-start(bf16[256,512]{1,0:T(8,128)(2,1)S(1)} %collective-permute-done.32.refs_5_) | copy-start | bytes 786436
  313.9 8.3 %collective-permute-start.15 = (bf16[256,512]{1,0:T(8,128)(2,1)}, bf16[256,512]{1,0:T(8,128)(2,1)S(1)}, u32[]{:S(2)}, u32[]{:S(2)}) collective-permute-start(bf16[256,512]{1,0:T(8,128)(2,1)} %get-tuple-element.96), channel_id=1, source_target_pairs={{0,1},{1,0},{2,3},{3,2},{4,5},{5,4},{6,7},{7,6},{8,9},{9,8},{10,11... | collective-permute-start | bytes 786440 | tf_op jit(solution)/shard_map/ppermute | solution.py:508
  322.1 164.6 %copy-start.8 = (bf16[256,512]{1,0:T(8,128)(2,1)}, bf16[256,512]{1,0:T(8,128)(2,1)S(1)}, u32[]{:S(2)}) copy-start(bf16[256,512]{1,0:T(8,128)(2,1)S(1)} %collective-permute-done.15.refs_11_) | copy-start | bytes 786436
  322.1 8.4 %collective-permute-start.16 = (bf16[256,512]{1,0:T(8,128)(2,1)S(1)}, bf16[256,512]{1,0:T(8,128)(2,1)S(1)}, u32[]{:S(2)}, u32[]{:S(2)}) collective-permute-start(bf16[256,512]{1,0:T(8,128)(2,1)S(1)} %copy-done.24), channel_id=1, source_target_pairs={{0,2},{1,3},{2,0},{3,1},{4,6},{5,7},{6,4},{7,5},{8,10},{9,11},{10,... | collective-permute-start | bytes 786440 | tf_op jit(solution)/shard_map/ppermute | solution.py:508
  330.5 156.3 %copy-start.9 = (bf16[256,512]{1,0:T(8,128)(2,1)}, bf16[256,512]{1,0:T(8,128)(2,1)S(1)}, u32[]{:S(2)}) copy-start(bf16[256,512]{1,0:T(8,128)(2,1)S(1)} %collective-permute-done.16.refs_12_) | copy-start | bytes 786436
  330.5 8.1 %collective-permute-start.17 = (bf16[256,512]{1,0:T(8,128)(2,1)S(1)}, bf16[256,512]{1,0:T(8,128)(2,1)S(1)}, u32[]{:S(2)}, u32[]{:S(2)}) collective-permute-start(bf16[256,512]{1,0:T(8,128)(2,1)S(1)} %copy-done.23), channel_id=1, source_target_pairs={{0,3},{1,2},{2,1},{3,0},{4,7},{5,6},{6,5},{7,4},{8,11},{9,10},{10,... | collective-permute-start | bytes 786440 | tf_op jit(solution)/shard_map/ppermute | solution.py:508
  338.6 148.2 %copy-start.10 = (bf16[256,512]{1,0:T(8,128)(2,1)}, bf16[256,512]{1,0:T(8,128)(2,1)S(1)}, u32[]{:S(2)}) copy-start(bf16[256,512]{1,0:T(8,128)(2,1)S(1)} %collective-permute-done.17.refs_13_) | copy-start | bytes 786436
  338.6 8.0 %collective-permute-start.10 = (bf16[256,512]{1,0:T(8,128)(2,1)}, bf16[256,512]{1,0:T(8,128)(2,1)S(1)}, u32[]{:S(2)}, u32[]{:S(2)}) collective-permute-start(bf16[256,512]{1,0:T(8,128)(2,1)} %get-tuple-element.85), channel_id=1, source_target_pairs={{0,2},{1,3},{2,0},{3,1},{4,6},{5,7},{6,4},{7,5},{8,10},{9,11},{10,... | collective-permute-start | bytes 786440 | tf_op jit(solution)/shard_map/ppermute | solution.py:508
  346.6 140.2 %copy-start.12 = (bf16[256,512]{1,0:T(8,128)(2,1)}, bf16[256,512]{1,0:T(8,128)(2,1)S(1)}, u32[]{:S(2)}) copy-start(bf16[256,512]{1,0:T(8,128)(2,1)S(1)} %collective-permute-done.10.refs_8_) | copy-start | bytes 786436
  346.6 8.8 %collective-permute-start.11 = (bf16[256,512]{1,0:T(8,128)(2,1)}, bf16[256,512]{1,0:T(8,128)(2,1)}, u32[]{:S(2)}, u32[]{:S(2)}) collective-permute-start(bf16[256,512]{1,0:T(8,128)(2,1)} %get-tuple-element.86), channel_id=1, source_target_pairs={{0,3},{1,2},{2,1},{3,0},{4,7},{5,6},{6,5},{7,4},{8,11},{9,10},{10,... | collective-permute-start | bytes 786440 | tf_op jit(solution)/shard_map/ppermute | solution.py:508
  355.4 59.9 %collective-permute-start.20 = (bf16[640,2048]{1,0:T(8,128)(2,1)}, bf16[640,2048]{1,0:T(8,128)(2,1)S(1)}, u32[]{:S(2)}, u32[]{:S(2)}) collective-permute-start(bf16[640,2048]{1,0:T(8,128)(2,1)} %collective-permute-done.19.refs_16_.refs_8_.refs_10_), channel_id=1, source_target_pairs={{0,4},{4,0},{8,12},{12,8},{1,5},{5,1},{9,13},{13,9},{2,6},{6,2},{1... | collective-permute-start | bytes 7864328 | tf_op jit(solution)/shard_map/ppermute | solution.py:511
  355.4 59.9 %collective-permute-start.23 = (bf16[640,2048]{1,0:T(8,128)(2,1)}, bf16[640,2048]{1,0:T(8,128)(2,1)S(1)}, u32[]{:S(2)}, u32[]{:S(2)}) collective-permute-start(bf16[640,2048]{1,0:T(8,128)(2,1)} %collective-permute-done.19.refs_16_.refs_8_.refs_10_), channel_id=1, source_target_pairs={{0,1},{1,0},{2,3},{3,2},{4,5},{5,4},{6,7},{7,6},{8,9},{9,8},{10,11... | collective-permute-start | bytes 7864328 | tf_op jit(solution)/shard_map/ppermute | solution.py:508
  356.1 120.9 %copy-start.1 = (bf16[640,2048]{1,0:T(8,128)(2,1)}, bf16[640,2048]{1,0:T(8,128)(2,1)S(1)}, u32[]{:S(2)}) copy-start(bf16[640,2048]{1,0:T(8,128)(2,1)S(1)} %collective-permute-done.21.refs_18_.refs_10_.refs_12_) | copy-start | bytes 7864324
  356.1 114.5 %collective-permute-start.22 = (bf16[640,2048]{1,0:T(8,128)(2,1)S(1)}, bf16[640,2048]{1,0:T(8,128)(2,1)S(1)}, u32[]{:S(2)}, u32[]{:S(2)}) collective-permute-start(bf16[640,2048]{1,0:T(8,128)(2,1)S(1)} %collective-permute-done.21.refs_18_.refs_10_.refs_12_), channel_id=1, source_target_pairs={{0,4},{4,0},{8,12},{12,8},{1,5},{5,1},{9,13},{13,9},{2,6},{6,2},{1... | collective-permute-start | bytes 7864328 | tf_op jit(solution)/shard_map/ppermute | solution.py:511
  415.4 55.3 %copy-start.2 = (bf16[640,2048]{1,0:T(8,128)(2,1)}, bf16[640,2048]{1,0:T(8,128)(2,1)S(1)}, u32[]{:S(2)}) copy-start(bf16[640,2048]{1,0:T(8,128)(2,1)S(1)} %collective-permute-done.20.refs_17_.refs_9_.refs_11_) | copy-start | bytes 7864324
  415.4 55.2 %collective-permute-start.25 = (bf16[640,2048]{1,0:T(8,128)(2,1)S(1)}, bf16[640,2048]{1,0:T(8,128)(2,1)S(1)}, u32[]{:S(2)}, u32[]{:S(2)}) collective-permute-start(bf16[640,2048]{1,0:T(8,128)(2,1)S(1)} %collective-permute-done.21.refs_18_.refs_10_.refs_12_), channel_id=1, source_target_pairs={{0,1},{1,0},{2,3},{3,2},{4,5},{5,4},{6,7},{7,6},{8,9},{9,8},{10,11... | collective-permute-start | bytes 7864328 | tf_op jit(solution)/shard_map/ppermute | solution.py:508
  415.4 56.2 %copy-start.3 = (bf16[640,2048]{1,0:T(8,128)(2,1)}, bf16[640,2048]{1,0:T(8,128)(2,1)S(1)}, u32[]{:S(2)}) copy-start(bf16[640,2048]{1,0:T(8,128)(2,1)S(1)} %collective-permute-done.23.refs_20_.refs_12_.refs_14_) | copy-start | bytes 7864324
  415.4 56.2 %collective-permute-start.24 = (bf16[640,2048]{1,0:T(8,128)(2,1)S(1)}, bf16[640,2048]{1,0:T(8,128)(2,1)S(1)}, u32[]{:S(2)}, u32[]{:S(2)}) collective-permute-start(bf16[640,2048]{1,0:T(8,128)(2,1)S(1)} %collective-permute-done.20.refs_17_.refs_9_.refs_11_), channel_id=1, source_target_pairs={{0,1},{1,0},{2,3},{3,2},{4,5},{5,4},{6,7},{7,6},{8,9},{9,8},{10,11... | collective-permute-start | bytes 7864328 | tf_op jit(solution)/shard_map/ppermute | solution.py:508
  470.6 4.9 collective-permute-start.26
  470.6 4.9 copy-start.5
  470.6 49.2 %collective-permute-start.35 = (bf16[2064,512]{1,0:T(8,128)(2,1)}, bf16[2064,512]{1,0:T(8,128)(2,1)}, u32[]{:S(2)}, u32[]{:S(2)}) collective-permute-start(bf16[2064,512]{1,0:T(8,128)(2,1)} %collective-permute-done.33.refs_2_), channel_id=1, source_target_pairs={{0,8},{4,12},{8,0},{12,4},{1,9},{5,13},{9,1},{13,5},{2,10},{6,14},... | collective-permute-start | bytes 6340616 | tf_op jit(solution)/shard_map/ppermute | solution.py:511
  471.6 93.1 %collective-permute-start.36 = (bf16[2064,512]{1,0:T(8,128)(2,1)}, bf16[2064,512]{1,0:T(8,128)(2,1)}, u32[]{:S(2)}, u32[]{:S(2)}) collective-permute-start(bf16[2064,512]{1,0:T(8,128)(2,1)} %collective-permute-done.34.refs_3_), channel_id=1, source_target_pairs={{0,8},{4,12},{8,0},{12,4},{1,9},{5,13},{9,1},{13,5},{2,10},{6,14},... | collective-permute-start | bytes 6340616 | tf_op jit(solution)/shard_map/ppermute | solution.py:511
  475.5 11.3 %collective-permute-start.9 = (bf16[256,512]{1,0:T(8,128)(2,1)}, bf16[256,512]{1,0:T(8,128)(2,1)}, u32[]{:S(2)}, u32[]{:S(2)}) collective-permute-start(bf16[256,512]{1,0:T(8,128)(2,1)} %get-tuple-element.84), channel_id=1, source_target_pairs={{0,1},{1,0},{2,3},{3,2},{4,5},{5,4},{6,7},{7,6},{8,9},{9,8},{10,11... | collective-permute-start | bytes 786440 | tf_op jit(solution)/shard_map/ppermute | solution.py:508
  486.8 19.1 %collective-permute-start.3 = (bf16[256,512]{1,0:T(8,128)(2,1)}, bf16[256,512]{1,0:T(8,128)(2,1)S(1)}, u32[]{:S(2)}, u32[]{:S(2)}) collective-permute-start(bf16[256,512]{1,0:T(8,128)(2,1)} %get-tuple-element.72), channel_id=1, source_target_pairs={{0,1},{1,0},{2,3},{3,2},{4,5},{5,4},{6,7},{7,6},{8,9},{9,8},{10,11... | collective-permute-start | bytes 786440 | tf_op jit(solution)/shard_map/ppermute | solution.py:508
  487.0 19.4 %collective-permute-start.4 = (bf16[256,512]{1,0:T(8,128)(2,1)}, bf16[256,512]{1,0:T(8,128)(2,1)S(1)}, u32[]{:S(2)}, u32[]{:S(2)}) collective-permute-start(bf16[256,512]{1,0:T(8,128)(2,1)} %get-tuple-element.73), channel_id=1, source_target_pairs={{0,2},{1,3},{2,0},{3,1},{4,6},{5,7},{6,4},{7,5},{8,10},{9,11},{10,... | collective-permute-start | bytes 786440 | tf_op jit(solution)/shard_map/ppermute | solution.py:508
  488.0 76.7 %collective-permute-start.5 = (bf16[256,512]{1,0:T(8,128)(2,1)}, bf16[256,512]{1,0:T(8,128)(2,1)S(1)}, u32[]{:S(2)}, u32[]{:S(2)}) collective-permute-start(bf16[256,512]{1,0:T(8,128)(2,1)} %get-tuple-element.74), channel_id=1, source_target_pairs={{0,3},{1,2},{2,1},{3,0},{4,7},{5,6},{6,5},{7,4},{8,11},{9,10},{10,... | collective-permute-start | bytes 786440 | tf_op jit(solution)/shard_map/ppermute | solution.py:508
  505.9 58.8 %copy-start.15 = (bf16[256,512]{1,0:T(8,128)(2,1)}, bf16[256,512]{1,0:T(8,128)(2,1)S(1)}, u32[]{:S(2)}) copy-start(bf16[256,512]{1,0:T(8,128)(2,1)S(1)} %collective-permute-done.3.refs_3_) | copy-start | bytes 786436
  505.9 115.5 %collective-permute-start.37 = (bf16[2064,512]{1,0:T(8,128)(2,1)}, bf16[2064,512]{1,0:T(8,128)(2,1)S(1)}, u32[]{:S(2)}, u32[]{:S(2)}) collective-permute-start(bf16[2064,512]{1,0:T(8,128)(2,1)} %collective-permute-done.33.refs_2_), channel_id=1, source_target_pairs={{0,1},{1,0},{2,3},{3,2},{4,5},{5,4},{6,7},{7,6},{8,9},{9,8},{10,11... | collective-permute-start | bytes 6340616 | tf_op jit(solution)/shard_map/ppermute | solution.py:508
  506.3 58.4 %copy-start.16 = (bf16[256,512]{1,0:T(8,128)(2,1)}, bf16[256,512]{1,0:T(8,128)(2,1)S(1)}, u32[]{:S(2)}) copy-start(bf16[256,512]{1,0:T(8,128)(2,1)S(1)} %collective-permute-done.4.refs_4_) | copy-start | bytes 786436
  506.3 115.1 %collective-permute-start.38 = (bf16[2064,512]{1,0:T(8,128)(2,1)}, bf16[2064,512]{1,0:T(8,128)(2,1)}, u32[]{:S(2)}, u32[]{:S(2)}) collective-permute-start(bf16[2064,512]{1,0:T(8,128)(2,1)} %collective-permute-done.34.refs_3_), channel_id=1, source_target_pairs={{0,1},{1,0},{2,3},{3,2},{4,5},{5,4},{6,7},{7,6},{8,9},{9,8},{10,11... | collective-permute-start | bytes 6340616 | tf_op jit(solution)/shard_map/ppermute | solution.py:508
  519.9 101.6 %collective-permute-start.39 = (bf16[2064,512]{1,0:T(8,128)(2,1)}, bf16[2064,512]{1,0:T(8,128)(2,1)}, u32[]{:S(2)}, u32[]{:S(2)}) collective-permute-start(bf16[2064,512]{1,0:T(8,128)(2,1)} %collective-permute-done.35.refs_4_), channel_id=1, source_target_pairs={{0,1},{1,0},{2,3},{3,2},{4,5},{5,4},{6,7},{7,6},{8,9},{9,8},{10,11... | collective-permute-start | bytes 6340616 | tf_op jit(solution)/shard_map/ppermute | solution.py:508
  564.7 56.8 %collective-permute-start.40 = (bf16[2064,512]{1,0:T(8,128)(2,1)}, bf16[2064,512]{1,0:T(8,128)(2,1)}, u32[]{:S(2)}, u32[]{:S(2)}) collective-permute-start(bf16[2064,512]{1,0:T(8,128)(2,1)} %collective-permute-done.36.refs_5_), channel_id=1, source_target_pairs={{0,1},{1,0},{2,3},{3,2},{4,5},{5,4},{6,7},{7,6},{8,9},{9,8},{10,11... | collective-permute-start | bytes 6340616 | tf_op jit(solution)/shard_map/ppermute | solution.py:508
  (5 other events, 9.6 us)

commit v2 on v1

--- a/solution.py
+++ b/solution.py
@@ -71,8 +71,8 @@
     return vec.astype(F32).reshape(1, -1)
 
 
-def ln1_kernel(seqs, x_ref, g_ref, lb_ref, bu_ref, up_ref, down_ref, wo_ref, *refs):
-    outs, (upq, downq, buf, ub, db, sems, isems, osems) = refs[:seqs], refs[seqs:]
+def ln1_kernel(seqs, idx_ref, x_ref, g_ref, lb_ref, bu_ref, up_ref, down_ref, wo_ref, *refs):
+    outs, (upq, downq, woq, buf, ub, db, sems, isems, osems) = refs[:seqs], refs[seqs:]
     seq = pl.program_id(0)
     dp = lax.axis_index("dp")
     feats, width = up_ref.shape[0], ub.shape[1]
@@ -81,7 +81,8 @@
     ins = [pltpu.make_async_copy(up_ref.at[:, cols(width)], ub.at[:feats], isems.at[0]),
            pltpu.make_async_copy(down_ref.at[cols(width)], db.at[:width], isems.at[1]),
            pltpu.make_async_copy(wo_ref.at[cols(few)], db.at[width:], isems.at[2])]
-    packs = [pltpu.make_async_copy(ub, upq, osems.at[0]), pltpu.make_async_copy(db, downq, osems.at[1])]
+    packs = [pltpu.make_async_copy(ub, upq, osems.at[0]), pltpu.make_async_copy(db.at[:width], downq, osems.at[1]),
+             pltpu.make_async_copy(db.at[width:], woq, osems.at[2])]
 
     @pl.when(seq == 0)
     def _():
@@ -108,23 +109,27 @@
             copy.wait()
 
 
-def ln1(x, g, b, bu, w_up, w_down, w_out, parts):
+def ln1(idx, x, g, b, bu, w_up, w_down, w_out, parts):
     seqs, tok, feats = x.shape
     up_t = jax.ShapeDtypeStruct((feats + 16, w_up.shape[1] // parts), BF16)
-    down_t = jax.ShapeDtypeStruct(((w_down.shape[0] + w_out.shape[0]) // parts, feats), BF16)
+    down_t = jax.ShapeDtypeStruct((w_down.shape[0] // parts, feats), BF16)
+    wo_t = jax.ShapeDtypeStruct((w_out.shape[0] // parts, feats), BF16)
     hbm = pl.BlockSpec(memory_space=pl.ANY)
     return pl.pallas_call(
         functools.partial(ln1_kernel, seqs),
-        grid=(seqs,),
-        in_specs=[pl.BlockSpec((1, tok, feats), lambda n: (n, 0, 0)), *[pl.BlockSpec(v.shape, lambda n: (0,)) for v in (g, b, bu)], hbm, hbm, hbm],
-        out_specs=[hbm] * (seqs + 2),
-        out_shape=[jax.ShapeDtypeStruct((tok, feats), BF16)] * seqs + [up_t, down_t],
-        scratch_shapes=[pltpu.VMEM((seqs, tok, feats), BF16), pltpu.VMEM(up_t.shape, BF16), pltpu.VMEM(down_t.shape, BF16),
-                        pltpu.SemaphoreType.DMA((seqs,)), pltpu.SemaphoreType.DMA((3,)), pltpu.SemaphoreType.DMA((2,))],
+        grid_spec=pltpu.PrefetchScalarGridSpec(
+            num_scalar_prefetch=1,
+            grid=(seqs,),
+            in_specs=[pl.BlockSpec((1, tok, feats), lambda n, s: (s[2 + n], 0, 0)), *[pl.BlockSpec(v.shape, lambda n, s: (0,)) for v in (g, b, bu)], hbm, hbm, hbm],
+            out_specs=[hbm] * (seqs + 3),
+            scratch_shapes=[pltpu.VMEM((seqs, tok, feats), BF16), pltpu.VMEM(up_t.shape, BF16), pltpu.VMEM((down_t.shape[0] + wo_t.shape[0], feats), BF16),
+                            pltpu.SemaphoreType.DMA((seqs,)), pltpu.SemaphoreType.DMA((3,)), pltpu.SemaphoreType.DMA((3,))],
+        ),
+        out_shape=[jax.ShapeDtypeStruct((tok, feats), BF16)] * seqs + [up_t, down_t, wo_t],
         compiler_params=pltpu.CompilerParams(vmem_limit_bytes=VMEM_BIG),
         cost_estimate=pl.CostEstimate(flops=int(2e9), bytes_accessed=x.size * 8, transcendentals=0),
         name="ln1",
-    )(x, g, b, bu, w_up, w_down, w_out)
+    )(idx, x, g, b, bu, w_up, w_down, w_out)
 
 
 def qkv_kernel(heads, hd, group, idx_ref, p0, p1, p2, p3, w_ref, b_ref,
@@ -189,9 +194,10 @@
     )(idx, *pieces, w, b)
 
 
-def attn_kernel(seq, heads, idx_ref, len_ref, slope_ref, q_ref, kn_ref, vn_ref, kt_ref, vt_ref, ki_ref, vi_ref,
+def attn_kernel(place, heads, idx_ref, len_ref, slope_ref, q_ref, kn_ref, vn_ref, kt_ref, vt_ref, ki_ref, vi_ref,
                 ko_in, vo_in, c0, c1, c2, c3, ko_ref, vo_ref, m_s, l_s, acc_s, stage, sems):
     head = pl.program_id(0)
+    seq = idx_ref[2 + place]
     length = len_ref[seq]
     chunk, hd = q_ref.shape[1], q_ref.shape[2]
 
@@ -290,19 +296,19 @@
             rows_out(n).wait()
 
 
-def attend(seq, idx, lens, slopes, q, kn, vn, kt, vt, ki, vi, ko, vo):
+def attend(place, idx, lens, slopes, q, kn, vn, kt, vt, ki, vi, ko, vo):
     heads, chunk, hd = q.shape
     toks = kt.shape[2]
     tok = chunk // 4
     per_head = pl.BlockSpec((1, chunk, hd), lambda h, *_: (h, 0, 0))
-    old = pl.BlockSpec((1, 1, toks, hd), lambda h, *_: (seq, h, 0, 0))
+    old = pl.BlockSpec((1, 1, toks, hd), lambda h, s, *_: (s[2 + place], h, 0, 0))
     hbm = pl.BlockSpec(memory_space=pl.ANY)
     piece = pl.BlockSpec((tok, hd), lambda h, *_: (0, h))
     piece_t = jax.ShapeDtypeStruct((tok, heads * hd), BF16)
     cache_t = jax.ShapeDtypeStruct(ko.shape, BF16)
     pairs = heads * chunk * (toks // 2 + chunk // 2)
     return pl.pallas_call(
-        functools.partial(attn_kernel, seq, heads),
+        functools.partial(attn_kernel, place, heads),
         grid_spec=pltpu.PrefetchScalarGridSpec(
             num_scalar_prefetch=3,
             grid=(heads,),
@@ -319,7 +325,7 @@
     )(idx, lens, slopes, q, kn, vn, kt, vt, ki, vi, ko, vo)
 
 
-def out_kernel(seqs, far_row, *refs):
+def out_kernel(seqs, *refs):
     refs = list(refs)
     take = lambda n: [refs.pop(0) for _ in range(n)]
     (idx_ref,) = take(1)
@@ -329,7 +335,7 @@
     tok = ctx[0][0].shape[0]
     part = near[0].shape[0]
     few = part // 4
-    copies = [pltpu.make_async_copy(xs.at[pl.ds(seqs[0], len(seqs))], xb, xsem)]
+    copies = [pltpu.make_async_copy(xs.at[idx_ref[2 + n]], xb.at[i], xsem.at[i]) for i, n in enumerate(seqs)]
     for i in range(len(seqs)):
         for k in range(4):
             copies.append(pltpu.make_async_copy(ctx[i][k], cb.at[i * tok:(i + 1) * tok, k * part:(k + 1) * part], csem.at[i, k]))
@@ -339,7 +345,7 @@
         parts.append([])
         for n in range(4):
             at = pl.ds(pl.multiple_of((a + 2) * part + (idx_ref[1] ^ n) * few, few), few)
-            parts[-1].append(pltpu.make_async_copy(far[a][n].at[far_row:far_row + few], wb.at[at], wsem.at[a + 2, n]))
+            parts[-1].append(pltpu.make_async_copy(far[a][n], wb.at[at], wsem.at[a + 2, n]))
     copies += [c for group in parts for c in group]
     for copy in copies:
         copy.start()
@@ -357,7 +363,7 @@
         n_ref[rows, :] = ln_rows(res, row_of(g_ref), row_of(lb_ref))
 
 
-def out_proj(idx, x, seqs, ctx, near, far, far_row, b, g, lb):
+def out_proj(idx, x, seqs, ctx, near, far, b, g, lb):
     tok, feats = x.shape[1:]
     rows = tok * len(seqs)
     flat = [c for got in ctx for c in got]
@@ -366,12 +372,12 @@
     t = jax.ShapeDtypeStruct((rows, feats), BF16)
     out = pl.BlockSpec((rows, feats), lambda n, s: (0, 0))
     return pl.pallas_call(
-        functools.partial(out_kernel, seqs, far_row),
+        functools.partial(out_kernel, seqs),
         grid_spec=pltpu.PrefetchScalarGridSpec(
             num_scalar_prefetch=1, grid=(1,),
             in_specs=[hbm] * (1 + len(flat) + 10) + [vec] * 3, out_specs=[out, out],
             scratch_shapes=[pltpu.VMEM((len(seqs), tok, feats), BF16), pltpu.VMEM((rows, feats), BF16), pltpu.VMEM((feats, feats), BF16),
-                            pltpu.VMEM((rows, feats), F32), pltpu.SemaphoreType.DMA, pltpu.SemaphoreType.DMA((len(seqs), 4)), pltpu.SemaphoreType.DMA((4, 4))],
+                            pltpu.VMEM((rows, feats), F32), pltpu.SemaphoreType.DMA((len(seqs),)), pltpu.SemaphoreType.DMA((len(seqs), 4)), pltpu.SemaphoreType.DMA((4, 4))],
         ),
         out_shape=[t, t],
         compiler_params=pltpu.CompilerParams(vmem_limit_bytes=VMEM_BIG),
@@ -383,6 +389,7 @@
 def mlp_kernel(near, groups, bias_row, *refs):
     refs = list(refs)
     take = lambda n: [refs.pop(0) for _ in range(n)]
+    (idx_ref,) = take(1)
     norms = take(groups)
     bias_refs = take(2) if near else None
     n_arr = 2 if near else 8
@@ -401,7 +408,7 @@
             cols = slice(i * width, (i + 1) * width)
             up, down = ups[a].at[:, cols], downs[a].at[cols, :]
         else:
-            up, down = ups[4 * a + i].at[:feats], downs[4 * a + i].at[:width]
+            up, down = ups[4 * a + i].at[:feats], downs[4 * a + i]
         copies = [pltpu.make_async_copy(down, dbuf.at[slot, a * width:(a + 1) * width], dsem.at[slot, a]),
                   pltpu.make_async_copy(up, ubuf.at[slot, a], usem.at[slot, a])]
         if not near:
@@ -469,13 +476,13 @@
             tok = out.shape[1]
             for n in range(out.shape[0]):
                 rows = slice(n * tok, (n + 1) * tok)
-                out[n] = (rb[rows, :].astype(F32) + acc[rows, :] + row_of(bd_ref)).astype(BF16)
-
-
-def mlp(norms, bias, ups, downs, width, seqs, acc=None, res=None, bd=None, bias_row=None):
+                out[idx_ref[2 + n]] = (rb[rows, :].astype(F32) + acc[rows, :] + row_of(bd_ref)).astype(BF16)
+
+
+def mlp(idx, norms, bias, ups, downs, width, seqs, acc=None, res=None, bd=None, bias_row=None):
     feats = norms[0].shape[1]
     rows = sum(a.shape[0] for a in norms)
-    whole = lambda a: pl.BlockSpec(a.shape, lambda n: (0,) * len(a.shape))
+    whole = lambda a: pl.BlockSpec(a.shape, lambda n, s: (0,) * len(a.shape))
     hbm = pl.BlockSpec(memory_space=pl.ANY)
     near = acc is None
     if near:
@@ -489,15 +496,17 @@
         out_spec = whole(out_t)
     return pl.pallas_call(
         functools.partial(mlp_kernel, near, len(norms), bias_row),
-        grid=(4,),
-        in_specs=specs, out_specs=out_spec, out_shape=out_t,
-        scratch_shapes=[pltpu.VMEM((rows, feats), BF16), pltpu.VMEM((16 if near else rows, feats), BF16), pltpu.VMEM((rows, feats), F32), pltpu.VMEM((2, 2, feats, width), BF16),
+        grid_spec=pltpu.PrefetchScalarGridSpec(
+            num_scalar_prefetch=1, grid=(4,), in_specs=specs, out_specs=out_spec,
+            scratch_shapes=[pltpu.VMEM((rows, feats), BF16), pltpu.VMEM((16 if near else rows, feats), BF16), pltpu.VMEM((rows, feats), F32), pltpu.VMEM((2, 2, feats, width), BF16),
                         pltpu.VMEM((2, 2 * width, feats), BF16), pltpu.VMEM((2, 2, 16, width), BF16), pltpu.SemaphoreType.DMA((len(norms),)), pltpu.SemaphoreType.DMA((len(norms),)),
                         pltpu.SemaphoreType.DMA((len(norms),)), pltpu.SemaphoreType.DMA((2, 2)), pltpu.SemaphoreType.DMA((2, 2)), pltpu.SemaphoreType.DMA((2, 2))],
+        ),
+        out_shape=out_t,
         compiler_params=pltpu.CompilerParams(vmem_limit_bytes=VMEM_BIG),
         cost_estimate=pl.CostEstimate(flops=4 * rows * feats * 8 * width, bytes_accessed=4 * feats * 8 * width, transcendentals=0),
         name="mlp",
-    )(*args)
+    )(idx, *args)
 
 
 def solution(mesh):
@@ -514,12 +523,15 @@
         seqs, tok, feats = x_local.shape
         cache_len, heads, hd = k_cache.shape[1:]
         tp, dp = lax.axis_index('tp'), lax.axis_index('dp')
-        idx = jnp.stack([tp, dp]).astype(jnp.int32)
+        before = (prefix_len[None, :] > prefix_len[:, None]) | ((prefix_len[None, :] == prefix_len[:, None]) & (jnp.arange(seqs)[None, :] < jnp.arange(seqs)[:, None]))
+        rank = jnp.sum(before.astype(jnp.int32), axis=1)
+        falling = jnp.sum(jnp.where(rank[None, :] == jnp.arange(seqs)[:, None], jnp.arange(seqs)[None, :], 0), axis=1)
+        idx = jnp.concatenate([jnp.stack([tp, dp]), falling]).astype(jnp.int32)
         head_ids = tp * heads + jnp.arange(heads)
         slopes = jnp.exp2(-8.0 * (head_ids + 1).astype(F32) / (heads * tp_size))
         near_bias = [b_up, tp_swap(b_up, 1)]
         wo_s = tp_swap(w_out, 1)
-        *normed, up_q, down_q = ln1(x_local, ln1_gain, ln1_bias, b_up, w_up, w_down, w_out, dp_size)
+        *normed, up_q, down_q, wo_q = ln1(idx, x_local, ln1_gain, ln1_bias, b_up, w_up, w_down, w_out, dp_size)
         x_x = [tp_swap(normed[b], 2) for b in range(seqs)]
         x_s = [tp_swap(normed[b], 1) for b in range(seqs)]
         x_xs = [tp_swap(x_x[b], 1) for b in range(seqs)]
@@ -536,6 +548,7 @@
 
         up_x, up_xs = spread(up_q, 1, 2)
         down_x, down_xs = spread(down_q, 2, 1)
+        wo_x, wo_xs = spread(wo_q, 1, 2)
         up_s, down_s = tp_swap(w_up, 1), tp_swap(w_down, 1)
 
         flat = (seqs, cache_len * heads, hd)
@@ -548,12 +561,12 @@
             *ctx, ko, vo = attend(b, idx, prefix_len, slopes, q, kn, vn, kt, vt, ki.reshape(inter), vi.reshape(inter), ko, vo)
             got.append([ctx[0]] + [tp_swap(ctx[k], k) for k in (1, 2, 3)])
         norms, resid, acc = [], [], []
-        for some in (tuple(range(seqs - 1)), (seqs - 1,)):
-            r, n2 = out_proj(idx, x_local, some, [got[b] for b in some], [w_out, wo_s], [down_x, down_xs], width, b_out, ln2_gain, ln2_bias)
+        for some in (tuple(range(seqs)),):
+            r, n2 = out_proj(idx, x_local, some, [got[b] for b in some], [w_out, wo_s], [wo_x, wo_xs], b_out, ln2_gain, ln2_bias)
             resid.append(r)
             norms.append(n2)
-            acc.append(mlp([n2], near_bias, [w_up, up_s], [w_down, down_s], width, seqs))
-        out = mlp(norms, None, up_x + up_xs, down_x + down_xs, width, seqs, acc, resid, b_down, feats)
+            acc.append(mlp(idx, [n2], near_bias, [w_up, up_s], [w_down, down_s], width, seqs))
+        out = mlp(idx, norms, None, up_x + up_xs, down_x + down_xs, width, seqs, acc, resid, b_down, feats)
         return out, ko, vo
 
     tok_spec = P('dp', 'tp', None)

time: 682 us -> 577 us (0.85)
  waiting for transfers between devices: 306 us -> 210 us
  Pallas kernels: 340 us -> 327 us
    ppermute x6 -> x9, waiting for transfers between devices: 171 us -> 109 us  [dp_swap(): return lax.ppermute(a, 'dp', [(i, i ^ k) for i in range(dp_size)])]
    ppermute x38 -> x43, waiting for transfers between devices: 135 us -> 101 us  [tp_swap(): return lax.ppermute(a, 'tp', [(i, i ^ k) for i in range(tp_size)])]
    pallas_call x3 -> x2, Pallas kernels: 105 us -> 97.8 us  [mlp(): pl.pallas_call(functools.partial(mlp_kernel, near, len(norms), bias_row),...]
    ppermute x38 -> x43, starting transfers between devices: 17.1 us -> 22.5 us  [tp_swap(): return lax.ppermute(a, 'tp', [(i, i ^ k) for i in range(tp_size)])]
    pallas_call x7 -> x6, Pallas kernels: 146 us -> 141 us  [the longest x4 109 us: attend(): pl.pallas_call(functools.partial(attn_kernel, place, heads), grid_spec=pl...]
  transfers between devices with their start and end apart: 44 -> 52, of which waited for: 16 -> 11; matrix products, arithmetic and copies ran while one was open for 0% -> 0% of each run, Pallas kernels for 42% -> 47%
where the time goes in v2:
time: 577 us; the launch traced here: 568 us
  Pallas kernels  327 us (57%)
  waiting for transfers between devices  210 us (36%)
  starting transfers between devices  25.9 us (4%)
    ppermute x9, waiting for transfers between devices, dp_swap(): return lax.ppermute(a, 'dp', [(i, i ^ k) for i in range(dp_size)])  109 us
    pallas_call x4, Pallas kernels, attend(): pl.pallas_call(functools.partial(attn_kernel, place, heads), grid_spec=pl...  109 us
    ppermute x43, waiting for transfers between devices, tp_swap(): return lax.ppermute(a, 'tp', [(i, i ^ k) for i in range(tp_size)])  101 us
    pallas_call x2, Pallas kernels, mlp(): pl.pallas_call(functools.partial(mlp_kernel, near, len(norms), bias_row),...  97.8 us
    pallas_call x4, Pallas kernels, qkv(): pl.pallas_call(functools.partial(qkv_kernel, heads, hd, group), grid_spec...  55.8 us
    pallas_call x1, Pallas kernels, prep(): pl.pallas_call(functools.partial(prep_kernel, heads), grid_spec=pltpu.Pre...  33 us
    ppermute x43, starting transfers between devices, tp_swap(): return lax.ppermute(a, 'tp', [(i, i ^ k) for i in range(tp_size)])  22.5 us
    pallas_call x1, Pallas kernels, out_proj(): pl.pallas_call(functools.partial(out_kernel, seqs), grid_spec=pltpu.Prefe...  22.2 us
  transfers between devices with their start and end apart: 52, of which 11 were waited for; matrix products, arithmetic and copies ran while one was open for 0% of the time, Pallas kernels for 47%

profile of v2, /device:TPU:0, one launch (start us, length us, event | category | flops | bytes accessed | tf_op | source)
XLA Modules:
  0.0 568.2 jit_solution(16163849071260333747)
XLA Ops:
  0.6 0.9 convert_reduce_fusion
  1.5 0.1 select_reduce_fusion
  1.7 0.7 pad_add_fusion.idx_ref.refs_0_
  2.3 9.9 %ln1.1 = (bf16[256,2048]{1,0:T(8,128)(2,1)}, bf16[256,2048]{1,0:T(8,128)(2,1)}, bf16[256,2048]{1,0:T(8,128)(2,1)}, bf16[256,2048]{1,0:T(8,128)(2,1)}, bf16[2064,...) custom-call(s32[6]{0:T(128)} %pad_add_fusion.idx_ref.refs_0_, ...), custom_call_target="tpu_custom_call" | custom-call | flops 2000000000 | bytes 16777216 | tf_op jit(solution)/shard_map/ln1/pallas_call | solution.py:118
  12.2 0.8 collective-permute-start
  13.0 2.5 collective-permute-start.1
  15.5 0.2 collective-permute-start.6
  15.7 0.3 collective-permute-start.7
  16.0 2.5 collective-permute-done.49.refs_3_
  18.5 1.4 collective-permute-start.25
  20.0 53.2 %collective-permute-done.25.refs_20_ = bf16[128,2048]{1,0:T(8,128)(2,1)S(1)} collective-permute-done((bf16[128,2048]{1,0:T(8,128)(2,1)}, bf16[128,2048]{1,0:T(8,128)(2,1)S(1)}, u32[]{:S(2)}, u32[]{:S(2)}) %collective-permute-start.25) | collective-permute-done | bytes 524320 | tf_op jit(solution)/shard_map/ppermute | solution.py:517
  73.2 1.8 collective-permute-start.13
  75.0 0.2 collective-permute-start.18
  75.2 0.8 collective-permute-start.19
  76.0 0.2 collective-permute-start.2
  76.2 33.0 %prep.1 = (bf16[4,16384,128]{2,1,0:T(8,128)(2,1)}, bf16[4,16384,128]{2,1,0:T(8,128)(2,1)}, bf16[4,4,4096,128]{3,2,1,0:T(8,128)(2,1)}, bf16[4,4,4096,128]{3,2,1,0:T(8,128)(2,1)}) custom-call(s32[4]{0:T(128)} %len_ref.9, bf16[4,16384,128]{2,1,0:T(8,128)(2,1)} %bitcast.24, bf16[4,16384,128]{2,1,0:T(8,128)(2,1)} %bitcast.25), custom_call_target="tpu_custom_call" | custom-call | flops 20000000000 | bytes 100663296 | tf_op jit(solution)/shard_map/prep/pallas_call | solution.py:53
  109.2 0.5 multiply_exponential_fusion.slope_ref
  109.7 0.8 collective-permute-start.26
  110.5 14.0 %qkv.4 = (bf16[4,1024,128]{2,1,0:T(8,128)(2,1)}, bf16[4,1024,128]{2,1,0:T(8,128)(2,1)}, bf16[4,1024,128]{2,1,0:T(8,128)(2,1)}, bf16[4096,128]{1,0:T(8,128)(2,1)}, bf16[4096,128]{1,0:T(8,128)(2,1)}) custom-call(s32[6]{0:T(128)} %pad_add_fusion.idx_ref.refs_0_, bf16[256,2048]{1,0:T(8,128)(2,1)} %get-tuple-element.60.p0, bf16[256,2048]{1,0:T(8,128)(2,1)} %copy-done.7, ...), custom_call_target="tpu_custom_call" | custom-call | flops 6442450944 | bytes 10485760 | tf_op jit(solution)/shard_map/qkv/pallas_call | solution.py:181
  124.5 0.7 collective-permute-start.27
  125.2 0.2 collective-permute-start.29
  125.5 1.4 collective-permute-start.28
  126.8 0.9 copy-done.5
  127.8 31.1 %attend.4 = (bf16[256,512]{1,0:T(8,128)(2,1)}, bf16[256,512]{1,0:T(8,128)(2,1)}, bf16[256,512]{1,0:T(8,128)(2,1)}, bf16[256,512]{1,0:T(8,128)(2,1)}, bf16[4,4096...) custom-call(s32[6]{0:T(128)} %pad_add_fusion.idx_ref.refs_0_, ...), custom_call_target="tpu_custom_call", output_to_operand_aliasing={{4}: (10, {}), {5}: (11, {})} | custom-call | flops 10737418240 | bytes 8388608 | tf_op jit(solution)/shard_map/attend/pallas_call | solution.py:310
  159.0 1.2 collective-permute-start.33
  160.3 0.8 collective-permute-start.41
  161.1 0.5 collective-permute-start.31
  161.6 13.9 %qkv.5 = (bf16[4,1024,128]{2,1,0:T(8,128)(2,1)}, bf16[4,1024,128]{2,1,0:T(8,128)(2,1)}, bf16[4,1024,128]{2,1,0:T(8,128)(2,1)}, bf16[4096,128]{1,0:T(8,128)(2,1)}, bf16[4096,128]{1,0:T(8,128)(2,1)}) custom-call(s32[6]{0:T(128)} %pad_add_fusion.idx_ref.refs_0_, bf16[256,2048]{1,0:T(8,128)(2,1)} %get-tuple-element.74.p0, ...), custom_call_target="tpu_custom_call" | custom-call | flops 6442450944 | bytes 10485760 | tf_op jit(solution)/shard_map/qkv/pallas_call | solution.py:181
  175.6 0.1 collective-permute-start.20
  175.6 28.4 %attend.5 = (bf16[256,512]{1,0:T(8,128)(2,1)}, bf16[256,512]{1,0:T(8,128)(2,1)}, bf16[256,512]{1,0:T(8,128)(2,1)}, bf16[256,512]{1,0:T(8,128)(2,1)}, bf16[4,4096...) custom-call(s32[6]{0:T(128)} %pad_add_fusion.idx_ref.refs_0_, ...), custom_call_target="tpu_custom_call", output_to_operand_aliasing={{4}: (10, {}), {5}: (11, {})} | custom-call | flops 10737418240 | bytes 8388608 | tf_op jit(solution)/shard_map/attend/pallas_call | solution.py:310
  204.1 0.5 collective-permute-start.32
  204.6 13.9 %qkv.6 = (bf16[4,1024,128]{2,1,0:T(8,128)(2,1)}, bf16[4,1024,128]{2,1,0:T(8,128)(2,1)}, bf16[4,1024,128]{2,1,0:T(8,128)(2,1)}, bf16[4096,128]{1,0:T(8,128)(2,1)}, bf16[4096,128]{1,0:T(8,128)(2,1)}) custom-call(s32[6]{0:T(128)} %pad_add_fusion.idx_ref.refs_0_, bf16[256,2048]{1,0:T(8,128)(2,1)} %get-tuple-element.86.p0, ...), custom_call_target="tpu_custom_call" | custom-call | flops 6442450944 | bytes 10485760 | tf_op jit(solution)/shard_map/qkv/pallas_call | solution.py:181
  218.5 0.1 collective-permute-start.50
  218.6 0.5 collective-permute-start.51
  219.1 33.5 %collective-permute-done.41.refs_10_ = bf16[512,2048]{1,0:T(8,128)(2,1)} collective-permute-done((bf16[512,2048]{1,0:T(8,128)(2,1)}, bf16[512,2048]{1,0:T(8,128)(2,1)}, u32[]{:S(2)}, u32[]{:S(2)}) %collective-permute-start.41) | collective-permute-done | bytes 2097184 | tf_op jit(solution)/shard_map/ppermute | solution.py:517
  252.7 1.1 collective-permute-start.4
  253.8 28.1 %attend.6 = (bf16[256,512]{1,0:T(8,128)(2,1)}, bf16[256,512]{1,0:T(8,128)(2,1)}, bf16[256,512]{1,0:T(8,128)(2,1)}, bf16[256,512]{1,0:T(8,128)(2,1)}, bf16[4,4096...) custom-call(s32[6]{0:T(128)} %pad_add_fusion.idx_ref.refs_0_, ...), custom_call_target="tpu_custom_call", output_to_operand_aliasing={{4}: (10, {}), {5}: (11, {})} | custom-call | flops 10737418240 | bytes 8388608 | tf_op jit(solution)/shard_map/attend/pallas_call | solution.py:310
  282.0 1.1 collective-permute-start.9
  283.0 1.1 collective-permute-start.10
  284.2 0.4 collective-permute-start.11
  284.5 14.0 %qkv.7 = (bf16[4,1024,128]{2,1,0:T(8,128)(2,1)}, bf16[4,1024,128]{2,1,0:T(8,128)(2,1)}, bf16[4,1024,128]{2,1,0:T(8,128)(2,1)}, bf16[4096,128]{1,0:T(8,128)(2,1)}, bf16[4096,128]{1,0:T(8,128)(2,1)}) custom-call(s32[6]{0:T(128)} %pad_add_fusion.idx_ref.refs_0_, bf16[256,2048]{1,0:T(8,128)(2,1)} %get-tuple-element.98.p0, bf16[256,2048]{1,0:T(8,128)(2,1)} %copy-done.4, ...), custom_call_target="tpu_custom_call" | custom-call | flops 6442450944 | bytes 10485760 | tf_op jit(solution)/shard_map/qkv/pallas_call | solution.py:181
  298.6 0.8 collective-permute-start.15
  299.4 1.1 collective-permute-start.16
  300.5 0.3 collective-permute-start.17
  300.8 21.0 %attend.7 = (bf16[256,512]{1,0:T(8,128)(2,1)}, bf16[256,512]{1,0:T(8,128)(2,1)}, bf16[256,512]{1,0:T(8,128)(2,1)}, bf16[256,512]{1,0:T(8,128)(2,1)}, bf16[4,4096...) custom-call(s32[6]{0:T(128)} %pad_add_fusion.idx_ref.refs_0_, ...), custom_call_target="tpu_custom_call", output_to_operand_aliasing={{4}: (10, {}), {5}: (11, {})} | custom-call | flops 10737418240 | bytes 8388608 | tf_op jit(solution)/shard_map/attend/pallas_call | solution.py:310
  321.9 0.8 collective-permute-start.21
  322.7 1.1 collective-permute-start.22
  323.8 0.3 collective-permute-start.23
  324.1 8.0 %collective-permute-done.22.refs_16_ = bf16[256,512]{1,0:T(8,128)(2,1)S(1)} collective-permute-done((bf16[256,512]{1,0:T(8,128)(2,1)}, bf16[256,512]{1,0:T(8,128)(2,1)S(1)}, u32[]{:S(2)}, u32[]{:S(2)}) %collective-permute-start.22) | collective-permute-done | bytes 262176 | tf_op jit(solution)/shard_map/ppermute | solution.py:517
  332.1 3.8 collective-permute-done.23.refs_17_
  335.9 1.1 collective-permute-start.45
  337.0 35.7 %collective-permute-done.42.refs_11_ = bf16[512,2048]{1,0:T(8,128)(2,1)} collective-permute-done((bf16[512,2048]{1,0:T(8,128)(2,1)}, bf16[512,2048]{1,0:T(8,128)(2,1)}, u32[]{:S(2)}, u32[]{:S(2)}) %collective-permute-start.42) | collective-permute-done | bytes 2097184 | tf_op jit(solution)/shard_map/ppermute | solution.py:520
  372.7 0.2 collective-permute-start.34
  372.9 5.4 collective-permute-done.43.refs_12_
  378.3 0.3 collective-permute-start.35
  378.6 42.0 %collective-permute-done.34.refs_3_ = bf16[2064,512]{1,0:T(8,128)(2,1)S(1)} collective-permute-done((bf16[2064,512]{1,0:T(8,128)(2,1)}, bf16[2064,512]{1,0:T(8,128)(2,1)S(1)}, u32[]{:S(2)}, u32[]{:S(2)}) %collective-permute-start.34) | collective-permute-done | bytes 2113568 | tf_op jit(solution)/shard_map/ppermute | solution.py:520
  420.7 5.0 collective-permute-done.35.refs_4_
  425.8 22.2 %outp.1 = (bf16[1024,2048]{1,0:T(8,128)(2,1)}, bf16[1024,2048]{1,0:T(8,128)(2,1)}) custom-call(s32[6]{0:T(128)} %pad_add_fusion.idx_ref.refs_0_, bf16[4,256,2048]{2,1,0:T(8,128)(2,1)} %refs_1_.1, bf16[256,512]{1,0:T(8,128)(2,1)} %get-tuple-element.70.refs_2_, bf16[256,512]{1,0:T(8,128)(2,1)} %copy-done.11, bf16[256,512]{1,0:T(8,128)(2,1)} %copy-done.12, ...), custom_call_target="tpu_custom_call" | custom-call | flops 8589934592 | bytes 8388608 | tf_op jit(solution)/shard_map/outp/pallas_call | solution.py:374
  447.9 20.7 %collective-permute-done.44.refs_13_ = bf16[512,2048]{1,0:T(8,128)(2,1)} collective-permute-done((bf16[512,2048]{1,0:T(8,128)(2,1)}, bf16[512,2048]{1,0:T(8,128)(2,1)}, u32[]{:S(2)}, u32[]{:S(2)}) %collective-permute-start.44) | collective-permute-done | bytes 2097184 | tf_op jit(solution)/shard_map/ppermute | solution.py:520
  468.6 0.5 collective-permute-start.38
  469.1 0.2 collective-permute-done.36.refs_5_
  469.4 0.5 collective-permute-start.48
  469.9 48.7 %mlp.2.refs_18_ = f32[1024,2048]{1,0:T(8,128)} custom-call(s32[6]{0:T(128)} %pad_add_fusion.idx_ref.refs_0_, bf16[1024,2048]{1,0:T(8,128)(2,1)} %get-tuple-element.111.refs_1_, bf16[2048]{0:T(1024)(128)(2,1)} %refs_2_.1, bf16[2048]{0:T(1024)(128)(2,1)} %copy-done.30, bf16[2048,2048]{1,0:T(8,128)(2,1)} %refs_4_.1, ...), custom_call_target="tpu_custom_call" | custom-call | flops 34359738368 | bytes 33554432 | tf_op jit(solution)/shard_map/mlp/pallas_call | solution.py:497
  518.7 49.1 %mlp.3 = bf16[4,256,2048]{2,1,0:T(8,128)(2,1)} custom-call(s32[6]{0:T(128)} %pad_add_fusion.idx_ref.refs_0_, bf16[1024,2048]{1,0:T(8,128)(2,1)} %get-tuple-element.111.refs_1_, bf16[2064,512]{1,0:T(8,128)(2,1)} %collective-permute-done.33.refs_2_, bf16[2064,512]{1,0:T(8,128)(2,1)} %copy-done.2, bf16[2064,512]{1,0:T(8,128)(2,1)} %collective-permute-done.35.refs_4_, ...), custom_call_target="tpu_custom_call" | custom-call | flops 34359738368 | bytes 33554432 | tf_op jit(solution)/shard_map/mlp/pallas_call | solution.py:497
  (119 shorter events, 0.5 us)
Async XLA Ops:
  12.2 61.0 %collective-permute-start = (bf16[256,2048]{1,0:T(8,128)(2,1)}, bf16[256,2048]{1,0:T(8,128)(2,1)S(1)}, u32[]{:S(2)}, u32[]{:S(2)}) collective-permute-start(bf16[256,2048]{1,0:T(8,128)(2,1)} %get-tuple-element.60.p0), channel_id=1, source_target_pairs={{0,1},{1,0},{2,3},{3,2},{4,5},{5,4},{6,7},{7,6},{8,9},{9,8},{10,11... | collective-permute-start | bytes 3145736 | tf_op jit(solution)/shard_map/ppermute | solution.py:517
  13.0 62.0 %collective-permute-start.1 = (bf16[256,2048]{1,0:T(8,128)(2,1)}, bf16[256,2048]{1,0:T(8,128)(2,1)}, u32[]{:S(2)}, u32[]{:S(2)}) collective-permute-start(bf16[256,2048]{1,0:T(8,128)(2,1)} %get-tuple-element.60.p0), channel_id=1, source_target_pairs={{0,2},{1,3},{2,0},{3,1},{4,6},{5,7},{6,4},{7,5},{8,10},{9,11},{10,... | collective-permute-start | bytes 3145736 | tf_op jit(solution)/shard_map/ppermute | solution.py:517
  15.5 59.7 %collective-permute-start.6 = (bf16[256,2048]{1,0:T(8,128)(2,1)}, bf16[256,2048]{1,0:T(8,128)(2,1)}, u32[]{:S(2)}, u32[]{:S(2)}) collective-permute-start(bf16[256,2048]{1,0:T(8,128)(2,1)} %get-tuple-element.74.p0), channel_id=1, source_target_pairs={{0,1},{1,0},{2,3},{3,2},{4,5},{5,4},{6,7},{7,6},{8,9},{9,8},{10,11... | collective-permute-start | bytes 3145736 | tf_op jit(solution)/shard_map/ppermute | solution.py:517
  15.7 60.3 %collective-permute-start.7 = (bf16[256,2048]{1,0:T(8,128)(2,1)}, bf16[256,2048]{1,0:T(8,128)(2,1)}, u32[]{:S(2)}, u32[]{:S(2)}) collective-permute-start(bf16[256,2048]{1,0:T(8,128)(2,1)} %get-tuple-element.74.p0), channel_id=1, source_target_pairs={{0,2},{1,3},{2,0},{3,1},{4,6},{5,7},{6,4},{7,5},{8,10},{9,11},{10,... | collective-permute-start | bytes 3145736 | tf_op jit(solution)/shard_map/ppermute | solution.py:517
  16.0 2.5 collective-permute-start.49
  18.5 90.7 %copy-start.30 = (bf16[2048]{0:T(1024)(128)(2,1)}, bf16[2048]{0:T(1024)(128)(2,1)S(1)}, u32[]{:S(2)}) copy-start(bf16[2048]{0:T(1024)(128)(2,1)S(1)} %collective-permute-done.49.refs_3_) | copy-start | bytes 12292
  18.5 54.7 %collective-permute-start.25 = (bf16[128,2048]{1,0:T(8,128)(2,1)}, bf16[128,2048]{1,0:T(8,128)(2,1)S(1)}, u32[]{:S(2)}, u32[]{:S(2)}) collective-permute-start(bf16[128,2048]{1,0:T(8,128)(2,1)} %get-tuple-element.110), channel_id=1, source_target_pairs={{0,2},{1,3},{2,0},{3,1},{4,6},{5,7},{6,4},{7,5},{8,10},{9,11},{10,... | collective-permute-start | bytes 1572872 | tf_op jit(solution)/shard_map/ppermute | solution.py:517
  73.2 52.0 %copy-start.8 = (bf16[128,2048]{1,0:T(8,128)(2,1)}, bf16[128,2048]{1,0:T(8,128)(2,1)S(1)}, u32[]{:S(2)}) copy-start(bf16[128,2048]{1,0:T(8,128)(2,1)S(1)} %collective-permute-done.25.refs_20_) | copy-start | bytes 1572868
  73.2 36.5 %collective-permute-start.12 = (bf16[256,2048]{1,0:T(8,128)(2,1)}, bf16[256,2048]{1,0:T(8,128)(2,1)}, u32[]{:S(2)}, u32[]{:S(2)}) collective-permute-start(bf16[256,2048]{1,0:T(8,128)(2,1)} %get-tuple-element.86.p0), channel_id=1, source_target_pairs={{0,1},{1,0},{2,3},{3,2},{4,5},{5,4},{6,7},{7,6},{8,9},{9,8},{10,11... | collective-permute-start | bytes 3145736 | tf_op jit(solution)/shard_map/ppermute | solution.py:517
  73.2 51.2 %collective-permute-start.13 = (bf16[256,2048]{1,0:T(8,128)(2,1)}, bf16[256,2048]{1,0:T(8,128)(2,1)}, u32[]{:S(2)}, u32[]{:S(2)}) collective-permute-start(bf16[256,2048]{1,0:T(8,128)(2,1)} %get-tuple-element.86.p0), channel_id=1, source_target_pairs={{0,2},{1,3},{2,0},{3,1},{4,6},{5,7},{6,4},{7,5},{8,10},{9,11},{10,... | collective-permute-start | bytes 3145736 | tf_op jit(solution)/shard_map/ppermute | solution.py:517
  75.0 50.2 %collective-permute-start.18 = (bf16[256,2048]{1,0:T(8,128)(2,1)}, bf16[256,2048]{1,0:T(8,128)(2,1)S(1)}, u32[]{:S(2)}, u32[]{:S(2)}) collective-permute-start(bf16[256,2048]{1,0:T(8,128)(2,1)} %get-tuple-element.98.p0), channel_id=1, source_target_pairs={{0,1},{1,0},{2,3},{3,2},{4,5},{5,4},{6,7},{7,6},{8,9},{9,8},{10,11... | collective-permute-start | bytes 3145736 | tf_op jit(solution)/shard_map/ppermute | solution.py:517
  75.2 51.6 %collective-permute-start.19 = (bf16[256,2048]{1,0:T(8,128)(2,1)}, bf16[256,2048]{1,0:T(8,128)(2,1)S(1)}, u32[]{:S(2)}, u32[]{:S(2)}) collective-permute-start(bf16[256,2048]{1,0:T(8,128)(2,1)} %get-tuple-element.98.p0), channel_id=1, source_target_pairs={{0,2},{1,3},{2,0},{3,1},{4,6},{5,7},{6,4},{7,5},{8,10},{9,11},{10,... | collective-permute-start | bytes 3145736 | tf_op jit(solution)/shard_map/ppermute | solution.py:517
  76.0 34.4 %collective-permute-start.2 = (bf16[256,2048]{1,0:T(8,128)(2,1)}, bf16[256,2048]{1,0:T(8,128)(2,1)}, u32[]{:S(2)}, u32[]{:S(2)}) collective-permute-start(bf16[256,2048]{1,0:T(8,128)(2,1)} %collective-permute-done.1.p2), channel_id=1, source_target_pairs={{0,1},{1,0},{2,3},{3,2},{4,5},{5,4},{6,7},{7,6},{8,9},{9,8},{10,11... | collective-permute-start | bytes 3145736 | tf_op jit(solution)/shard_map/ppermute | solution.py:517
  109.7 15.7 %collective-permute-start.26 = (bf16[128,2048]{1,0:T(8,128)(2,1)S(1)}, bf16[128,2048]{1,0:T(8,128)(2,1)}, u32[]{:S(2)}, u32[]{:S(2)}) collective-permute-start(bf16[128,2048]{1,0:T(8,128)(2,1)S(1)} %collective-permute-done.25.refs_20_), channel_id=1, source_target_pairs={{0,4},{4,0},{8,12},{12,8},{1,5},{5,1},{9,13},{13,9},{2,6},{6,2},{1... | collective-permute-start | bytes 1572872 | tf_op jit(solution)/shard_map/ppermute | solution.py:520
  110.5 50.6 %collective-permute-start.8 = (bf16[256,2048]{1,0:T(8,128)(2,1)}, bf16[256,2048]{1,0:T(8,128)(2,1)}, u32[]{:S(2)}, u32[]{:S(2)}) collective-permute-start(bf16[256,2048]{1,0:T(8,128)(2,1)} %collective-permute-done.7.p2), channel_id=1, source_target_pairs={{0,1},{1,0},{2,3},{3,2},{4,5},{5,4},{6,7},{7,6},{8,9},{9,8},{10,11... | collective-permute-start | bytes 3145736 | tf_op jit(solution)/shard_map/ppermute | solution.py:517
  124.5 34.5 %collective-permute-start.27 = (bf16[128,2048]{1,0:T(8,128)(2,1)S(1)}, bf16[128,2048]{1,0:T(8,128)(2,1)}, u32[]{:S(2)}, u32[]{:S(2)}) collective-permute-start(bf16[128,2048]{1,0:T(8,128)(2,1)S(1)} %collective-permute-done.25.refs_20_), channel_id=1, source_target_pairs={{0,8},{4,12},{8,0},{12,4},{1,9},{5,13},{9,1},{13,5},{2,10},{6,14},... | collective-permute-start | bytes 1572872 | tf_op jit(solution)/shard_map/ppermute | solution.py:520
  125.2 33.8 %collective-permute-start.29 = (bf16[128,2048]{1,0:T(8,128)(2,1)S(1)}, bf16[128,2048]{1,0:T(8,128)(2,1)}, u32[]{:S(2)}, u32[]{:S(2)}) collective-permute-start(bf16[128,2048]{1,0:T(8,128)(2,1)S(1)} %collective-permute-done.25.refs_20_), channel_id=1, source_target_pairs={{0,1},{1,0},{2,3},{3,2},{4,5},{5,4},{6,7},{7,6},{8,9},{9,8},{10,11... | collective-permute-start | bytes 1572872 | tf_op jit(solution)/shard_map/ppermute | solution.py:517
  125.5 34.8 %collective-permute-start.28 = (bf16[128,2048]{1,0:T(8,128)(2,1)}, bf16[128,2048]{1,0:T(8,128)(2,1)}, u32[]{:S(2)}, u32[]{:S(2)}) collective-permute-start(bf16[128,2048]{1,0:T(8,128)(2,1)} %collective-permute-done.26.refs_21_), channel_id=1, source_target_pairs={{0,8},{4,12},{8,0},{12,4},{1,9},{5,13},{9,1},{13,5},{2,10},{6,14},... | collective-permute-start | bytes 1572872 | tf_op jit(solution)/shard_map/ppermute | solution.py:520
  126.8 34.3 %collective-permute-start.30 = (bf16[128,2048]{1,0:T(8,128)(2,1)}, bf16[128,2048]{1,0:T(8,128)(2,1)}, u32[]{:S(2)}, u32[]{:S(2)}) collective-permute-start(bf16[128,2048]{1,0:T(8,128)(2,1)} %collective-permute-done.26.refs_21_), channel_id=1, source_target_pairs={{0,1},{1,0},{2,3},{3,2},{4,5},{5,4},{6,7},{7,6},{8,9},{9,8},{10,11... | collective-permute-start | bytes 1572872 | tf_op jit(solution)/shard_map/ppermute | solution.py:517
  159.0 59.6 %collective-permute-start.24 = (bf16[512,2048]{1,0:T(8,128)(2,1)S(1)}, bf16[512,2048]{1,0:T(8,128)(2,1)}, u32[]{:S(2)}, u32[]{:S(2)}) collective-permute-start(bf16[512,2048]{1,0:T(8,128)(2,1)S(1)} %copy-done), channel_id=1, source_target_pairs={{0,1},{1,0},{2,3},{3,2},{4,5},{5,4},{6,7},{7,6},{8,9},{9,8},{10,11... | collective-permute-start | bytes 6291464 | tf_op jit(solution)/shard_map/ppermute | solution.py:517
  159.0 94.7 %collective-permute-start.33 = (bf16[2064,512]{1,0:T(8,128)(2,1)}, bf16[2064,512]{1,0:T(8,128)(2,1)}, u32[]{:S(2)}, u32[]{:S(2)}) collective-permute-start(bf16[2064,512]{1,0:T(8,128)(2,1)} %get-tuple-element.112), channel_id=1, source_target_pairs={{0,2},{1,3},{2,0},{3,1},{4,6},{5,7},{6,4},{7,5},{8,10},{9,11},{10,... | collective-permute-start | bytes 6340616 | tf_op jit(solution)/shard_map/ppermute | solution.py:517
  160.3 92.4 %collective-permute-start.41 = (bf16[512,2048]{1,0:T(8,128)(2,1)}, bf16[512,2048]{1,0:T(8,128)(2,1)}, u32[]{:S(2)}, u32[]{:S(2)}) collective-permute-start(bf16[512,2048]{1,0:T(8,128)(2,1)} %get-tuple-element.113), channel_id=1, source_target_pairs={{0,2},{1,3},{2,0},{3,1},{4,6},{5,7},{6,4},{7,5},{8,10},{9,11},{10,... | collective-permute-start | bytes 6291464 | tf_op jit(solution)/shard_map/ppermute | solution.py:517
  161.1 42.9 %collective-permute-start.14 = (bf16[256,2048]{1,0:T(8,128)(2,1)}, bf16[256,2048]{1,0:T(8,128)(2,1)}, u32[]{:S(2)}, u32[]{:S(2)}) collective-permute-start(bf16[256,2048]{1,0:T(8,128)(2,1)} %collective-permute-done.13.p2), channel_id=1, source_target_pairs={{0,1},{1,0},{2,3},{3,2},{4,5},{5,4},{6,7},{7,6},{8,9},{9,8},{10,11... | collective-permute-start | bytes 3145736 | tf_op jit(solution)/shard_map/ppermute | solution.py:517
  161.1 14.4 %collective-permute-start.31 = (bf16[128,2048]{1,0:T(8,128)(2,1)}, bf16[128,2048]{1,0:T(8,128)(2,1)S(1)}, u32[]{:S(2)}, u32[]{:S(2)}) collective-permute-start(bf16[128,2048]{1,0:T(8,128)(2,1)} %collective-permute-done.27.refs_22_), channel_id=1, source_target_pairs={{0,1},{1,0},{2,3},{3,2},{4,5},{5,4},{6,7},{7,6},{8,9},{9,8},{10,11... | collective-permute-start | bytes 1572872 | tf_op jit(solution)/shard_map/ppermute | solution.py:517
  175.6 42.9 %collective-permute-start.20 = (bf16[256,2048]{1,0:T(8,128)(2,1)S(1)}, bf16[256,2048]{1,0:T(8,128)(2,1)}, u32[]{:S(2)}, u32[]{:S(2)}) collective-permute-start(bf16[256,2048]{1,0:T(8,128)(2,1)S(1)} %copy-done.6), channel_id=1, source_target_pairs={{0,1},{1,0},{2,3},{3,2},{4,5},{5,4},{6,7},{7,6},{8,9},{9,8},{10,11... | collective-permute-start | bytes 3145736 | tf_op jit(solution)/shard_map/ppermute | solution.py:517
  204.0 49.7 %copy-start.17 = (bf16[256,512]{1,0:T(8,128)(2,1)S(1)}, bf16[256,512]{1,0:T(8,128)(2,1)}, u32[]{:S(2)}) copy-start(bf16[256,512]{1,0:T(8,128)(2,1)} %get-tuple-element.73) | copy-start | bytes 786436
  204.1 15.0 %collective-permute-start.32 = (bf16[128,2048]{1,0:T(8,128)(2,1)}, bf16[128,2048]{1,0:T(8,128)(2,1)S(1)}, u32[]{:S(2)}, u32[]{:S(2)}) collective-permute-start(bf16[128,2048]{1,0:T(8,128)(2,1)} %collective-permute-done.28.refs_23_), channel_id=1, source_target_pairs={{0,1},{1,0},{2,3},{3,2},{4,5},{5,4},{6,7},{7,6},{8,9},{9,8},{10,11... | collective-permute-start | bytes 1572872 | tf_op jit(solution)/shard_map/ppermute | solution.py:517
  218.5 250.9 %collective-permute-start.50 = (bf16[2048,2048]{1,0:T(8,128)(2,1)}, bf16[2048,2048]{1,0:T(8,128)(2,1)}, u32[]{:S(2)}, u32[]{:S(2)}) collective-permute-start(bf16[2048,2048]{1,0:T(8,128)(2,1)} %refs_4_.1), channel_id=1, source_target_pairs={{0,1},{1,0},{2,3},{3,2},{4,5},{5,4},{6,7},{7,6},{8,9},{9,8},{10,11... | collective-permute-start | bytes 25165832 | tf_op jit(solution)/shard_map/ppermute | solution.py:517
  218.6 251.3 %collective-permute-start.51 = (bf16[2048,2048]{1,0:T(8,128)(2,1)}, bf16[2048,2048]{1,0:T(8,128)(2,1)}, u32[]{:S(2)}, u32[]{:S(2)}) collective-permute-start(bf16[2048,2048]{1,0:T(8,128)(2,1)} %refs_6_.1), channel_id=1, source_target_pairs={{0,1},{1,0},{2,3},{3,2},{4,5},{5,4},{6,7},{7,6},{8,9},{9,8},{10,11... | collective-permute-start | bytes 25165832 | tf_op jit(solution)/shard_map/ppermute | solution.py:517
  219.1 62.9 %copy-start.10 = (bf16[128,2048]{1,0:T(8,128)(2,1)}, bf16[128,2048]{1,0:T(8,128)(2,1)S(1)}, u32[]{:S(2)}) copy-start(bf16[128,2048]{1,0:T(8,128)(2,1)S(1)} %collective-permute-done.32.refs_27_) | copy-start | bytes 1572868
  219.1 62.9 %collective-permute-start.3 = (bf16[256,512]{1,0:T(8,128)(2,1)}, bf16[256,512]{1,0:T(8,128)(2,1)S(1)}, u32[]{:S(2)}, u32[]{:S(2)}) collective-permute-start(bf16[256,512]{1,0:T(8,128)(2,1)} %get-tuple-element.71), channel_id=1, source_target_pairs={{0,1},{1,0},{2,3},{3,2},{4,5},{5,4},{6,7},{7,6},{8,9},{9,8},{10,11... | collective-permute-start | bytes 786440 | tf_op jit(solution)/shard_map/ppermute | solution.py:517
  252.7 30.4 %collective-permute-start.4 = (bf16[256,512]{1,0:T(8,128)(2,1)}, bf16[256,512]{1,0:T(8,128)(2,1)S(1)}, u32[]{:S(2)}, u32[]{:S(2)}) collective-permute-start(bf16[256,512]{1,0:T(8,128)(2,1)} %get-tuple-element.72), channel_id=1, source_target_pairs={{0,2},{1,3},{2,0},{3,1},{4,6},{5,7},{6,4},{7,5},{8,10},{9,11},{10,... | collective-permute-start | bytes 786440 | tf_op jit(solution)/shard_map/ppermute | solution.py:517
  253.7 30.4 %collective-permute-start.5 = (bf16[256,512]{1,0:T(8,128)(2,1)S(1)}, bf16[256,512]{1,0:T(8,128)(2,1)S(1)}, u32[]{:S(2)}, u32[]{:S(2)}) collective-permute-start(bf16[256,512]{1,0:T(8,128)(2,1)S(1)} %copy-done.17), channel_id=1, source_target_pairs={{0,3},{1,2},{2,1},{3,0},{4,7},{5,6},{6,5},{7,4},{8,11},{9,10},{10,... | collective-permute-start | bytes 786440 | tf_op jit(solution)/shard_map/ppermute | solution.py:517
  282.0 16.6 %collective-permute-start.9 = (bf16[256,512]{1,0:T(8,128)(2,1)S(1)}, bf16[256,512]{1,0:T(8,128)(2,1)S(1)}, u32[]{:S(2)}, u32[]{:S(2)}) collective-permute-start(bf16[256,512]{1,0:T(8,128)(2,1)S(1)} %copy-done.23), channel_id=1, source_target_pairs={{0,1},{1,0},{2,3},{3,2},{4,5},{5,4},{6,7},{7,6},{8,9},{9,8},{10,11... | collective-permute-start | bytes 786440 | tf_op jit(solution)/shard_map/ppermute | solution.py:517
  283.0 16.3 %collective-permute-start.10 = (bf16[256,512]{1,0:T(8,128)(2,1)S(1)}, bf16[256,512]{1,0:T(8,128)(2,1)S(1)}, u32[]{:S(2)}, u32[]{:S(2)}) collective-permute-start(bf16[256,512]{1,0:T(8,128)(2,1)S(1)} %copy-done.22), channel_id=1, source_target_pairs={{0,2},{1,3},{2,0},{3,1},{4,6},{5,7},{6,4},{7,5},{8,10},{9,11},{10,... | collective-permute-start | bytes 786440 | tf_op jit(solution)/shard_map/ppermute | solution.py:517
  284.2 16.3 %collective-permute-start.11 = (bf16[256,512]{1,0:T(8,128)(2,1)S(1)}, bf16[256,512]{1,0:T(8,128)(2,1)S(1)}, u32[]{:S(2)}, u32[]{:S(2)}) collective-permute-start(bf16[256,512]{1,0:T(8,128)(2,1)S(1)} %copy-done.21), channel_id=1, source_target_pairs={{0,3},{1,2},{2,1},{3,0},{4,7},{5,6},{6,5},{7,4},{8,11},{9,10},{10,... | collective-permute-start | bytes 786440 | tf_op jit(solution)/shard_map/ppermute | solution.py:517
  298.6 23.3 %collective-permute-start.15 = (bf16[256,512]{1,0:T(8,128)(2,1)S(1)}, bf16[256,512]{1,0:T(8,128)(2,1)S(1)}, u32[]{:S(2)}, u32[]{:S(2)}) collective-permute-start(bf16[256,512]{1,0:T(8,128)(2,1)S(1)} %copy-done.29), channel_id=1, source_target_pairs={{0,1},{1,0},{2,3},{3,2},{4,5},{5,4},{6,7},{7,6},{8,9},{9,8},{10,11... | collective-permute-start | bytes 786440 | tf_op jit(solution)/shard_map/ppermute | solution.py:517
  299.4 23.3 %collective-permute-start.16 = (bf16[256,512]{1,0:T(8,128)(2,1)S(1)}, bf16[256,512]{1,0:T(8,128)(2,1)S(1)}, u32[]{:S(2)}, u32[]{:S(2)}) collective-permute-start(bf16[256,512]{1,0:T(8,128)(2,1)S(1)} %copy-done.28), channel_id=1, source_target_pairs={{0,2},{1,3},{2,0},{3,1},{4,6},{5,7},{6,4},{7,5},{8,10},{9,11},{10,... | collective-permute-start | bytes 786440 | tf_op jit(solution)/shard_map/ppermute | solution.py:517
  300.5 23.3 %collective-permute-start.17 = (bf16[256,512]{1,0:T(8,128)(2,1)S(1)}, bf16[256,512]{1,0:T(8,128)(2,1)S(1)}, u32[]{:S(2)}, u32[]{:S(2)}) collective-permute-start(bf16[256,512]{1,0:T(8,128)(2,1)S(1)} %copy-done.26), channel_id=1, source_target_pairs={{0,3},{1,2},{2,1},{3,0},{4,7},{5,6},{6,5},{7,4},{8,11},{9,10},{10,... | collective-permute-start | bytes 786440 | tf_op jit(solution)/shard_map/ppermute | solution.py:517
  321.9 103.8 %copy-start.18 = (bf16[256,512]{1,0:T(8,128)(2,1)}, bf16[256,512]{1,0:T(8,128)(2,1)S(1)}, u32[]{:S(2)}) copy-start(bf16[256,512]{1,0:T(8,128)(2,1)S(1)} %collective-permute-done.15.refs_11_) | copy-start | bytes 786436
  321.9 2.2 collective-permute-start.21
  322.7 103.0 %copy-start.19 = (bf16[256,512]{1,0:T(8,128)(2,1)}, bf16[256,512]{1,0:T(8,128)(2,1)S(1)}, u32[]{:S(2)}) copy-start(bf16[256,512]{1,0:T(8,128)(2,1)S(1)} %collective-permute-done.16.refs_12_) | copy-start | bytes 786436
  322.7 9.4 %collective-permute-start.22 = (bf16[256,512]{1,0:T(8,128)(2,1)}, bf16[256,512]{1,0:T(8,128)(2,1)S(1)}, u32[]{:S(2)}, u32[]{:S(2)}) collective-permute-start(bf16[256,512]{1,0:T(8,128)(2,1)} %get-tuple-element.108), channel_id=1, source_target_pairs={{0,2},{1,3},{2,0},{3,1},{4,6},{5,7},{6,4},{7,5},{8,10},{9,11},{10,... | collective-permute-start | bytes 786440 | tf_op jit(solution)/shard_map/ppermute | solution.py:517
  323.8 102.0 %copy-start.20 = (bf16[256,512]{1,0:T(8,128)(2,1)}, bf16[256,512]{1,0:T(8,128)(2,1)S(1)}, u32[]{:S(2)}) copy-start(bf16[256,512]{1,0:T(8,128)(2,1)S(1)} %collective-permute-done.17.refs_13_) | copy-start | bytes 786436
  323.8 12.1 %collective-permute-start.23 = (bf16[256,512]{1,0:T(8,128)(2,1)}, bf16[256,512]{1,0:T(8,128)(2,1)S(1)}, u32[]{:S(2)}, u32[]{:S(2)}) collective-permute-start(bf16[256,512]{1,0:T(8,128)(2,1)} %get-tuple-element.109), channel_id=1, source_target_pairs={{0,3},{1,2},{2,1},{3,0},{4,7},{5,6},{6,5},{7,4},{8,11},{9,10},{10,... | collective-permute-start | bytes 786440 | tf_op jit(solution)/shard_map/ppermute | solution.py:517
  324.1 101.6 %copy-start.24 = (bf16[256,512]{1,0:T(8,128)(2,1)}, bf16[256,512]{1,0:T(8,128)(2,1)S(1)}, u32[]{:S(2)}) copy-start(bf16[256,512]{1,0:T(8,128)(2,1)S(1)} %collective-permute-done.21.refs_15_) | copy-start | bytes 786436
  324.1 48.6 %collective-permute-start.42 = (bf16[512,2048]{1,0:T(8,128)(2,1)}, bf16[512,2048]{1,0:T(8,128)(2,1)}, u32[]{:S(2)}, u32[]{:S(2)}) collective-permute-start(bf16[512,2048]{1,0:T(8,128)(2,1)} %collective-permute-done.41.refs_10_), channel_id=1, source_target_pairs={{0,4},{4,0},{8,12},{12,8},{1,5},{5,1},{9,13},{13,9},{2,6},{6,2},{1... | collective-permute-start | bytes 6291464 | tf_op jit(solution)/shard_map/ppermute | solution.py:520
  332.1 93.7 %copy-start.25 = (bf16[256,512]{1,0:T(8,128)(2,1)}, bf16[256,512]{1,0:T(8,128)(2,1)S(1)}, u32[]{:S(2)}) copy-start(bf16[256,512]{1,0:T(8,128)(2,1)S(1)} %collective-permute-done.22.refs_16_) | copy-start | bytes 786436
  332.1 46.3 %collective-permute-start.43 = (bf16[512,2048]{1,0:T(8,128)(2,1)}, bf16[512,2048]{1,0:T(8,128)(2,1)}, u32[]{:S(2)}, u32[]{:S(2)}) collective-permute-start(bf16[512,2048]{1,0:T(8,128)(2,1)} %collective-permute-done.41.refs_10_), channel_id=1, source_target_pairs={{0,8},{4,12},{8,0},{12,4},{1,9},{5,13},{9,1},{13,5},{2,10},{6,14},... | collective-permute-start | bytes 6291464 | tf_op jit(solution)/shard_map/ppermute | solution.py:520
  335.9 89.9 %copy-start.27 = (bf16[256,512]{1,0:T(8,128)(2,1)}, bf16[256,512]{1,0:T(8,128)(2,1)S(1)}, u32[]{:S(2)}) copy-start(bf16[256,512]{1,0:T(8,128)(2,1)S(1)} %collective-permute-done.23.refs_17_) | copy-start | bytes 786436
  335.9 42.7 %collective-permute-start.45 = (bf16[512,2048]{1,0:T(8,128)(2,1)}, bf16[512,2048]{1,0:T(8,128)(2,1)S(1)}, u32[]{:S(2)}, u32[]{:S(2)}) collective-permute-start(bf16[512,2048]{1,0:T(8,128)(2,1)} %collective-permute-done.41.refs_10_), channel_id=1, source_target_pairs={{0,1},{1,0},{2,3},{3,2},{4,5},{5,4},{6,7},{7,6},{8,9},{9,8},{10,11... | collective-permute-start | bytes 6291464 | tf_op jit(solution)/shard_map/ppermute | solution.py:517
  372.7 48.0 %collective-permute-start.34 = (bf16[2064,512]{1,0:T(8,128)(2,1)}, bf16[2064,512]{1,0:T(8,128)(2,1)S(1)}, u32[]{:S(2)}, u32[]{:S(2)}) collective-permute-start(bf16[2064,512]{1,0:T(8,128)(2,1)} %collective-permute-done.33.refs_2_), channel_id=1, source_target_pairs={{0,4},{4,0},{8,12},{12,8},{1,5},{5,1},{9,13},{13,9},{2,6},{6,2},{1... | collective-permute-start | bytes 6340616 | tf_op jit(solution)/shard_map/ppermute | solution.py:520
  378.3 47.4 %collective-permute-start.35 = (bf16[2064,512]{1,0:T(8,128)(2,1)}, bf16[2064,512]{1,0:T(8,128)(2,1)}, u32[]{:S(2)}, u32[]{:S(2)}) collective-permute-start(bf16[2064,512]{1,0:T(8,128)(2,1)} %collective-permute-done.33.refs_2_), channel_id=1, source_target_pairs={{0,8},{4,12},{8,0},{12,4},{1,9},{5,13},{9,1},{13,5},{2,10},{6,14},... | collective-permute-start | bytes 6340616 | tf_op jit(solution)/shard_map/ppermute | solution.py:520
  378.6 42.0 %copy-start.3 = (bf16[512,2048]{1,0:T(8,128)(2,1)}, bf16[512,2048]{1,0:T(8,128)(2,1)S(1)}, u32[]{:S(2)}) copy-start(bf16[512,2048]{1,0:T(8,128)(2,1)S(1)} %collective-permute-done.45.refs_14_) | copy-start | bytes 6291460
  378.6 47.1 %collective-permute-start.37 = (bf16[2064,512]{1,0:T(8,128)(2,1)}, bf16[2064,512]{1,0:T(8,128)(2,1)}, u32[]{:S(2)}, u32[]{:S(2)}) collective-permute-start(bf16[2064,512]{1,0:T(8,128)(2,1)} %collective-permute-done.33.refs_2_), channel_id=1, source_target_pairs={{0,1},{1,0},{2,3},{3,2},{4,5},{5,4},{6,7},{7,6},{8,9},{9,8},{10,11... | collective-permute-start | bytes 6340616 | tf_op jit(solution)/shard_map/ppermute | solution.py:517
  420.6 48.0 %copy-start.2 = (bf16[2064,512]{1,0:T(8,128)(2,1)}, bf16[2064,512]{1,0:T(8,128)(2,1)S(1)}, u32[]{:S(2)}) copy-start(bf16[2064,512]{1,0:T(8,128)(2,1)S(1)} %collective-permute-done.34.refs_3_) | copy-start | bytes 6340612
  420.6 48.7 %collective-permute-start.36 = (bf16[2064,512]{1,0:T(8,128)(2,1)S(1)}, bf16[2064,512]{1,0:T(8,128)(2,1)}, u32[]{:S(2)}, u32[]{:S(2)}) collective-permute-start(bf16[2064,512]{1,0:T(8,128)(2,1)S(1)} %collective-permute-done.34.refs_3_), channel_id=1, source_target_pairs={{0,8},{4,12},{8,0},{12,4},{1,9},{5,13},{9,1},{13,5},{2,10},{6,14},... | collective-permute-start | bytes 6340616 | tf_op jit(solution)/shard_map/ppermute | solution.py:520
  425.7 42.9 %collective-permute-start.44 = (bf16[512,2048]{1,0:T(8,128)(2,1)}, bf16[512,2048]{1,0:T(8,128)(2,1)}, u32[]{:S(2)}, u32[]{:S(2)}) collective-permute-start(bf16[512,2048]{1,0:T(8,128)(2,1)} %collective-permute-done.43.refs_12_), channel_id=1, source_target_pairs={{0,4},{4,0},{8,12},{12,8},{1,5},{5,1},{9,13},{13,9},{2,6},{6,2},{1... | collective-permute-start | bytes 6291464 | tf_op jit(solution)/shard_map/ppermute | solution.py:520
  425.7 42.9 %collective-permute-start.46 = (bf16[512,2048]{1,0:T(8,128)(2,1)}, bf16[512,2048]{1,0:T(8,128)(2,1)}, u32[]{:S(2)}, u32[]{:S(2)}) collective-permute-start(bf16[512,2048]{1,0:T(8,128)(2,1)} %collective-permute-done.42.refs_11_), channel_id=1, source_target_pairs={{0,1},{1,0},{2,3},{3,2},{4,5},{5,4},{6,7},{7,6},{8,9},{9,8},{10,11... | collective-permute-start | bytes 6291464 | tf_op jit(solution)/shard_map/ppermute | solution.py:517
  468.6 50.0 %collective-permute-start.47 = (bf16[512,2048]{1,0:T(8,128)(2,1)}, bf16[512,2048]{1,0:T(8,128)(2,1)}, u32[]{:S(2)}, u32[]{:S(2)}) collective-permute-start(bf16[512,2048]{1,0:T(8,128)(2,1)} %collective-permute-done.43.refs_12_), channel_id=1, source_target_pairs={{0,1},{1,0},{2,3},{3,2},{4,5},{5,4},{6,7},{7,6},{8,9},{9,8},{10,11... | collective-permute-start | bytes 6291464 | tf_op jit(solution)/shard_map/ppermute | solution.py:517
  468.6 50.0 %collective-permute-start.38 = (bf16[2064,512]{1,0:T(8,128)(2,1)S(1)}, bf16[2064,512]{1,0:T(8,128)(2,1)}, u32[]{:S(2)}, u32[]{:S(2)}) collective-permute-start(bf16[2064,512]{1,0:T(8,128)(2,1)S(1)} %collective-permute-done.34.refs_3_), channel_id=1, source_target_pairs={{0,1},{1,0},{2,3},{3,2},{4,5},{5,4},{6,7},{7,6},{8,9},{9,8},{10,11... | collective-permute-start | bytes 6340616 | tf_op jit(solution)/shard_map/ppermute | solution.py:517
  469.4 49.3 %collective-permute-start.39 = (bf16[2064,512]{1,0:T(8,128)(2,1)}, bf16[2064,512]{1,0:T(8,128)(2,1)}, u32[]{:S(2)}, u32[]{:S(2)}) collective-permute-start(bf16[2064,512]{1,0:T(8,128)(2,1)} %collective-permute-done.35.refs_4_), channel_id=1, source_target_pairs={{0,1},{1,0},{2,3},{3,2},{4,5},{5,4},{6,7},{7,6},{8,9},{9,8},{10,11... | collective-permute-start | bytes 6340616 | tf_op jit(solution)/shard_map/ppermute | solution.py:517
  469.4 49.3 %collective-permute-start.48 = (bf16[512,2048]{1,0:T(8,128)(2,1)}, bf16[512,2048]{1,0:T(8,128)(2,1)}, u32[]{:S(2)}, u32[]{:S(2)}) collective-permute-start(bf16[512,2048]{1,0:T(8,128)(2,1)} %collective-permute-done.44.refs_13_), channel_id=1, source_target_pairs={{0,1},{1,0},{2,3},{3,2},{4,5},{5,4},{6,7},{7,6},{8,9},{9,8},{10,11... | collective-permute-start | bytes 6291464 | tf_op jit(solution)/shard_map/ppermute | solution.py:517
  469.9 48.8 %collective-permute-start.40 = (bf16[2064,512]{1,0:T(8,128)(2,1)}, bf16[2064,512]{1,0:T(8,128)(2,1)}, u32[]{:S(2)}, u32[]{:S(2)}) collective-permute-start(bf16[2064,512]{1,0:T(8,128)(2,1)} %collective-permute-done.36.refs_5_), channel_id=1, source_target_pairs={{0,1},{1,0},{2,3},{3,2},{4,5},{5,4},{6,7},{7,6},{8,9},{9,8},{10,11... | collective-permute-start | bytes 6340616 | tf_op jit(solution)/shard_map/ppermute | solution.py:517
  (19 other events, 372.7 us)
